TPU v7x, 8 devices: a whole 2x2x1 slice. The times are simulated.
8 devices in a mesh: rep: 2 (over y, z), dp: 4 (over x, core).
Axes of the slice: x: 2, y: 2, z: 1, core: 2. Of those that a mesh axis runs over, the one named last changes fastest.
Arguments:
- g_w_gate: bfloat16 [8, 2, 1024, 3072], P(('rep', 'dp')), parts along dimension 0
- g_w_up: bfloat16 [8, 2, 1024, 3072], P(('rep', 'dp')), parts along dimension 0
- g_w_down: bfloat16 [8, 2, 3072, 1024], P(('rep', 'dp')), parts along dimension 0
- w_gate: bfloat16 [2, 1024, 3072], replicated
- w_up: bfloat16 [2, 1024, 3072], replicated
- w_down: bfloat16 [2, 3072, 1024], replicated
- m_w_gate: float32 [2, 1024, 3072], P(None, 'dp')
- m_w_up: float32 [2, 1024, 3072], P(None, 'dp')
- m_w_down: float32 [2, 3072, 1024], P(None, 'dp')
- v_w_gate: float32 [2, 1024, 3072], P(None, 'dp')
- v_w_up: float32 [2, 1024, 3072], P(None, 'dp')
- v_w_down: float32 [2, 3072, 1024], P(None, 'dp')
Outputs:
- output 1: bfloat16 [4, 1024, 3072], P('rep'), parts along dimension 0
- output 2: bfloat16 [4, 1024, 3072], P('rep'), parts along dimension 0
- output 3: bfloat16 [4, 3072, 1024], P('rep'), parts along dimension 0
- output 4: float32 [4, 1024, 3072], P('rep', 'dp'), parts along dimension 0
- output 5: float32 [4, 1024, 3072], P('rep', 'dp'), parts along dimension 0
- output 6: float32 [4, 3072, 1024], P('rep', 'dp'), parts along dimension 0
- output 7: float32 [4, 1024, 3072], P('rep', 'dp'), parts along dimension 0
- output 8: float32 [4, 1024, 3072], P('rep', 'dp'), parts along dimension 0
- output 9: float32 [4, 3072, 1024], P('rep', 'dp'), parts along dimension 0
There are 2 independent parts. A program takes and returns all parts, laid end to end along the dimension named above; an argument that names none is the same for every part.
All inputs are finite; a program needn't handle non-finite values.
Results may differ from a plain program's by a relative error of at most 0.022.
Values are sent between devices in bfloat16 or wider.
A program may use at most 2 GiB of HBM per device.

v0:
```python
import functools
import math

import jax
import jax.numpy as jnp
from jax import lax
from jax.experimental import pallas as pl
from jax.experimental.pallas import tpu as pltpu
from jax.sharding import PartitionSpec as P


ACROSS = [(0, 2), (2, 0), (1, 3), (3, 1)]
BESIDE = [(0, 1), (1, 0), (2, 3), (3, 2)]

SUMS = (
    (0, 0, 0, 32), (0, 0, 32, 32), (0, 0, 64, 64), (0, 0, 128, 128), (0, 1, 0, 256),
    (1, 0, 0, 256), (1, 1, 0, 256), (2, 0, 0, 768), (2, 1, 0, 768),
)
CHUNKS = (
    (0, 0, 0, 256), (0, 1, 0, 256), (1, 0, 0, 256), (1, 1, 0, 256),
    (2, 0, 0, 768), (2, 1, 0, 384), (2, 1, 384, 192), (2, 1, 576, 96), (2, 1, 672, 48), (2, 1, 720, 48),
)
STEPS = tuple(
    (r, c, max(sums[2], chunk[2]), min(sums[3], chunk[3]))
    for r, sums in enumerate(SUMS)
    for c, chunk in enumerate(CHUNKS)
    if sums[:2] == chunk[:2] and sums[2] < chunk[2] + chunk[3] and chunk[2] < sums[2] + sums[3]
)
LAST = len(CHUNKS) - 1
MESH = pl.DeviceIdType.MESH


def pair_body(chunk, nears, *refs):
    n = len(nears)
    terms, (both, *near_refs) = refs[:3], refs[3 : 4 + n]
    got, mine, total, got_send, got_recv, in_sem, out_sem, near_send, near_recv = refs[4 + n :]
    which, layer, first, rows = chunk
    me = lax.axis_index("dp")
    partner = {"dp": me ^ 1}
    barrier = pltpu.get_barrier_semaphore()
    pl.semaphore_signal(barrier, inc=1, device_id=partner, device_id_type=MESH)

    def block(which, layer, first, rows, owner):
        size = terms[which].shape[2] // 4
        return terms[which].at[0, layer, pl.ds(pl.multiple_of(owner * size + first, 16), rows)]

    tile = pair_tile(rows, terms[which].shape[3])
    count = rows // tile
    owns = [
        pltpu.make_async_copy(block(which, layer, first + t * tile, tile, me ^ 2), mine.at[pl.ds(t * tile, tile)], in_sem.at[t])
        for t in range(count)
    ]
    fars = [
        pltpu.make_async_remote_copy(
            block(which, layer, first + t * tile, tile, me ^ 3), got.at[pl.ds(t * tile, tile)],
            got_send.at[t], got_recv.at[t], device_id=partner, device_id_type=MESH)
        for t in range(count)
    ]
    beside = [
        pltpu.make_async_remote_copy(
            block(*SUMS[c], me ^ 1), near_refs[i], near_send.at[i], near_recv.at[i], device_id=partner, device_id_type=MESH)
        for i, c in enumerate(nears)
    ]
    outs = [pltpu.make_async_copy(total.at[pl.ds(t * tile, tile)], both.at[pl.ds(t * tile, tile)], out_sem.at[t]) for t in range(count)]
    pl.semaphore_wait(barrier, 1)
    for far, own in zip(fars, owns):
        far.start()
        own.start()
    for copy in beside:
        copy.start()
    for t in range(count):
        owns[t].wait()
        fars[t].wait_recv()
        here = pl.ds(t * tile, tile)
        total[here] = (got[here].astype(jnp.float32) + mine[here].astype(jnp.float32)).astype(jnp.bfloat16)
        outs[t].start()
    for t in range(count):
        fars[t].wait_send()
        outs[t].wait()
    for copy in beside:
        copy.wait()


def first_pair_body(chunk, terms, both, got, mine, send_sem, recv_sem, in_sem):
    _, layer, first, rows = chunk
    me = lax.axis_index("dp")
    partner = {"dp": me ^ 1}
    barrier = pltpu.get_barrier_semaphore()
    pl.semaphore_signal(barrier, inc=1, device_id=partner, device_id_type=MESH)

    def block(owner):
        size = terms.shape[2] // 4
        return terms.at[0, layer, pl.ds(pl.multiple_of(owner * size + first, 16), rows)]

    own = pltpu.make_async_copy(block(me ^ 2), mine, in_sem)
    far = pltpu.make_async_remote_copy(block(me ^ 3), got, send_sem, recv_sem, device_id=partner, device_id_type=MESH)
    own.start()
    pl.semaphore_wait(barrier, 1)
    far.start()
    own.wait()
    far.wait_recv()
    both[...] = (got[...].astype(jnp.float32) + mine[...].astype(jnp.float32)).astype(jnp.bfloat16)
    far.wait_send()


def first_pair(terms):
    which, _, _, rows = SUMS[0]
    cols = terms[which].shape[3]
    return pl.pallas_call(
        functools.partial(first_pair_body, SUMS[0]),
        in_specs=[pl.BlockSpec(memory_space=pltpu.HBM)],
        out_specs=pl.BlockSpec(memory_space=pltpu.VMEM),
        out_shape=jax.ShapeDtypeStruct((rows, cols), jnp.bfloat16),
        scratch_shapes=[pltpu.VMEM((rows, cols), jnp.bfloat16)] * 2 + [pltpu.SemaphoreType.DMA] * 3,
        compiler_params=pltpu.CompilerParams(collective_id=0, has_side_effects=True, vmem_limit_bytes=52 * 2**20),
        cost_estimate=pl.CostEstimate(flops=rows * cols, bytes_accessed=8 * rows * cols, transcendentals=0),
        name="first_pair",
    )(terms[which])


def pair_tile(rows, cols):
    return rows if rows * cols <= 96 * 3072 else math.gcd(rows, 64 * 3072 // cols)


def pair(terms, index, nears):
    chunk = SUMS[index]
    which, _, _, rows = chunk
    cols = terms[which].shape[3]
    count = rows // pair_tile(rows, cols)
    anywhere = pl.BlockSpec(memory_space=pl.ANY)
    shapes = [(rows, cols)] + [(SUMS[c][3], terms[SUMS[c][0]].shape[3]) for c in nears]
    return pl.pallas_call(
        functools.partial(pair_body, chunk, nears),
        in_specs=[anywhere] * 3,
        out_specs=[anywhere] * len(shapes),
        out_shape=[jax.ShapeDtypeStruct(shape, jnp.bfloat16) for shape in shapes],
        scratch_shapes=[pltpu.VMEM((rows, cols), jnp.bfloat16)] * 3
        + [pltpu.SemaphoreType.DMA((count,))] * 4
        + [pltpu.SemaphoreType.DMA((max(1, len(nears)),))] * 2,
        compiler_params=pltpu.CompilerParams(collective_id=index, has_side_effects=True),
        cost_estimate=pl.CostEstimate(flops=rows * cols, bytes_accessed=10 * rows * cols, transcendentals=0),
        name="pair",
    )(*terms)


def adamw_body(n_alias, me, own, near, far, w, m, v, *rest):
    send, out, m_out, v_out = rest[n_alias:]
    g = own[...].astype(jnp.float32) + near[...].astype(jnp.float32) + far[...].astype(jnp.float32)
    g = g.reshape(m.shape).astype(jnp.bfloat16).astype(jnp.float32)
    m_new = 0.9 * m[...] + 0.1 * g
    v_new = 0.95 * v[...] + 0.05 * g * g
    w_old = w[...].astype(jnp.float32)
    new = (w_old - 0.02 * (m_new * lax.rsqrt(v_new + 1e-8) + 0.1 * w_old)).astype(jnp.bfloat16)
    send[...] = new.reshape(send.shape)
    out[...] = new
    m_out[...] = m_new
    v_out[...] = v_new


def adamw(me, terms, near, far, w, m, v, step, before):
    r, c, first, rows = step
    _, layer, sum_first, _ = SUMS[r]
    _, _, chunk_first, chunk_rows = CHUNKS[c]
    block, cols = m.shape[1], m.shape[2]
    tile = math.gcd(rows, first, block, first - sum_first, first - chunk_first, 128 * 3072 // cols)
    at, per = first // tile, block // tile
    of_sum, of_chunk = (first - sum_first) // tile, (first - chunk_first) // tile
    mine = pl.BlockSpec((1, tile, cols), lambda i, me: (layer, at + i, 0))
    whole = pl.BlockSpec((1, tile, cols), lambda i, me: (layer, me[0] * per + at + i, 0))
    term = pl.BlockSpec((1, 1, tile, cols), lambda i, me: (0, layer, me[0] * per + at + i, 0))
    sums = pl.BlockSpec((tile, cols), lambda i, me: (of_sum + i, 0))
    chunk = pl.BlockSpec((tile, cols), lambda i, me: (of_chunk + i, 0))
    anywhere = pl.BlockSpec(memory_space=pl.ANY)
    have = [i for i, array in enumerate(before) if array is not None]
    size = rows * cols
    return pl.pallas_call(
        functools.partial(adamw_body, len(have)),
        grid_spec=pltpu.PrefetchScalarGridSpec(
            num_scalar_prefetch=1,
            grid=(rows // tile,),
            in_specs=[term, sums, sums, whole, mine, mine] + [anywhere] * len(have),
            out_specs=[chunk, whole, mine, mine],
        ),
        out_shape=[
            jax.ShapeDtypeStruct((chunk_rows, cols), jnp.bfloat16),
            jax.ShapeDtypeStruct(w.shape, jnp.bfloat16),
            jax.ShapeDtypeStruct(m.shape, jnp.float32),
            jax.ShapeDtypeStruct(v.shape, jnp.float32),
        ],
        input_output_aliases={7 + n: i for n, i in enumerate(have)},
        cost_estimate=pl.CostEstimate(flops=14 * size, bytes_accessed=28 * size, transcendentals=size),
        name="adamw",
    )(me, terms, near, far, w, m, v, *(before[i] for i in have))


def place_body(what, block, me, *refs):
    pieces, (_, out, sem) = refs[:-3], refs[-3:]
    copies = []
    for i, ((c, other), src) in enumerate(zip(what, pieces, strict=True)):
        _, layer, first, rows = CHUNKS[c]
        to = out.at[layer, pl.ds(pl.multiple_of((me[0] ^ other) * block + first, 16), rows)]
        copies.append(pltpu.make_async_copy(src, to, sem.at[i]))
    for copy in copies:
        copy.start()
    for copy in copies:
        copy.wait()


def place(me, what, pieces, out, block):
    size = sum(piece.size for piece in pieces)
    anywhere = pl.BlockSpec(memory_space=pl.ANY)
    n = len(pieces)
    return pl.pallas_call(
        functools.partial(place_body, what, block),
        in_specs=[pl.BlockSpec(memory_space=pltpu.SMEM)] + [pl.BlockSpec(memory_space=pltpu.VMEM)] * n + [anywhere],
        out_specs=anywhere,
        out_shape=jax.ShapeDtypeStruct(out.shape, out.dtype),
        input_output_aliases={1 + n: 0},
        scratch_shapes=[pltpu.SemaphoreType.DMA((n,))],
        compiler_params=pltpu.CompilerParams(vmem_limit_bytes=16 * 2**20),
        cost_estimate=pl.CostEstimate(flops=size, bytes_accessed=4 * size, transcendentals=0),
        name="place",
    )(me, *pieces, out)


def carry_body(chunk, block, me, beside, across, corner, before, out, held, in_sem, out_sem):
    _, layer, first, rows = chunk
    ins = [pltpu.make_async_copy(src, held.at[i], in_sem.at[i]) for i, src in enumerate((beside, across, corner))]
    outs = [
        pltpu.make_async_copy(held.at[i], out.at[layer, pl.ds(pl.multiple_of((me[0] ^ (1 + i)) * block + first, 16), rows)], out_sem.at[i])
        for i in range(3)
    ]
    for copy in ins:
        copy.start()
    for came, goes in zip(ins, outs):
        came.wait()
        goes.start()
    for copy in outs:
        copy.wait()


def carry(me, chunk, pieces, out, block):
    _, _, _, rows = chunk
    cols = out.shape[2]
    anywhere = pl.BlockSpec(memory_space=pl.ANY)
    return pl.pallas_call(
        functools.partial(carry_body, chunk, block),
        in_specs=[pl.BlockSpec(memory_space=pltpu.SMEM)] + [anywhere] * 4,
        out_specs=anywhere,
        out_shape=jax.ShapeDtypeStruct(out.shape, out.dtype),
        input_output_aliases={4: 0},
        scratch_shapes=[
            pltpu.VMEM((3, rows, cols), jnp.bfloat16),
            pltpu.SemaphoreType.DMA((3,)),
            pltpu.SemaphoreType.DMA((3,)),
        ],
        cost_estimate=pl.CostEstimate(flops=3 * rows * cols, bytes_accessed=12 * rows * cols, transcendentals=0),
        name="carry",
    )(me, *pieces, out)


def solution(mesh):
    def inner(*arrays):
        terms, weights, m, v = (arrays[i : i + 3] for i in (0, 3, 6, 9))
        me = lax.axis_index("dp").astype(jnp.int32).reshape(1)

        def send(x, to):
            return lax.ppermute(x, "dp", to)

        arrived, near = [], []
        for r in range(len(SUMS)):
            both, *more = pair(terms, r, () if r < 3 else (0, 1, 2, 3) if r == 3 else (r,)) if r else (first_pair(terms),)
            near += more
            arrived.append(send(both, ACROSS))

        state = [[None] * 3 for _ in weights]
        new = [None] * len(CHUNKS)
        for step in STEPS:
            r, c, _, _ = step
            which = SUMS[r][0]
            new[c], *state[which] = adamw(
                me, terms[which], near[r], arrived[r], weights[which], m[which], v[which], step, (new[c], *state[which]))
        across, beside, corner = [], [], []
        for c in range(len(CHUNKS)):
            across.append(send(new[c], ACROSS))
            beside.append(send(new[c], BESIDE))
        for c in range(len(CHUNKS)):
            corner.append(send(across[c], BESIDE))
        came = {1: beside, 2: across, 3: corner}
        for c in range(LAST):
            which = CHUNKS[c][0]
            what = ((c, 1), (c, 2), (c, 3))
            if c == LAST - 2:
                what += ((LAST - 1, 1), (LAST, 1))
            if c == LAST - 1:
                what = ((c, 2), (c, 3), (LAST, 2))
            pieces = [came[other][i] for i, other in what]
            if c < LAST - 2:
                state[which][0] = carry(me, CHUNKS[c], pieces, state[which][0], m[which].shape[1])
            else:
                state[which][0] = place(me, what, pieces, state[which][0], m[which].shape[1])
        which, layer, first, _ = CHUNKS[LAST]
        row = (lax.axis_index("dp") ^ 3) * m[which].shape[1] + first
        state[which][0] = lax.dynamic_update_slice(state[which][0], corner[LAST][None], (layer, row, 0))
        return tuple(state[which][i] for i in range(3) for which in range(3))

    all_of, cut_rows = P(None, None, None), P(None, "dp", None)
    return jax.shard_map(
        inner,
        mesh=mesh,
        in_specs=(P(("rep", "dp"), None, None, None),) * 3 + (all_of,) * 3 + (cut_rows,) * 6,
        out_specs=(P("rep", None, None),) * 3 + (P("rep", "dp", None),) * 6,
        check_vma=False,
    )
```

profile of v0, /device:TPU:0, one launch (start us, length us, event | category | flops | bytes accessed | tf_op | source)
XLA Modules:
  0.0 461.6 jit_solution(2988679443132305522)
XLA Ops:
  0.6 6.6 %pair.15 = (bf16[768,1024]{1,0:T(8,128)(2,1)}, bf16[768,1024]{1,0:T(8,128)(2,1)}) custom-call(bf16[1,2,1024,3072]{3,2,1,0:T(8,128)(2,1)} %refs_0_.15, bf16[1,2,1024,3072]{3,2,1,0:T(8,128)(2,1)} %refs_1_.15, bf16[1,2,3072,1024]{3,2,1,0:T(8,128)(2,1)} %own.25), custom_call_target="tpu_custom_call" | custom-call | flops 786432 | bytes 7864320 | tf_op jit(solution)/shard_map/pair/pallas_call | solution.py:132
  7.3 2.9 collective-permute-start.20
  10.2 6.2 %pair.14 = (bf16[768,1024]{1,0:T(8,128)(2,1)}, bf16[768,1024]{1,0:T(8,128)(2,1)}) custom-call(bf16[1,2,1024,3072]{3,2,1,0:T(8,128)(2,1)} %refs_0_.15, bf16[1,2,1024,3072]{3,2,1,0:T(8,128)(2,1)} %refs_1_.15, bf16[1,2,3072,1024]{3,2,1,0:T(8,128)(2,1)} %own.25), custom_call_target="tpu_custom_call" | custom-call | flops 786432 | bytes 7864320 | tf_op jit(solution)/shard_map/pair/pallas_call | solution.py:132
  16.4 1.7 first_pair.1
  18.1 2.0 collective-permute-start.4
  20.1 2.4 pair.11
  22.6 6.2 %pair.13 = (bf16[256,3072]{1,0:T(8,128)(2,1)}, bf16[256,3072]{1,0:T(8,128)(2,1)}) custom-call(bf16[1,2,1024,3072]{3,2,1,0:T(8,128)(2,1)} %refs_0_.15, bf16[1,2,1024,3072]{3,2,1,0:T(8,128)(2,1)} %refs_1_.15, bf16[1,2,3072,1024]{3,2,1,0:T(8,128)(2,1)} %own.25), custom_call_target="tpu_custom_call" | custom-call | flops 786432 | bytes 7864320 | tf_op jit(solution)/shard_map/pair/pallas_call | solution.py:132
  28.8 2.0 collective-permute-start.12
  30.8 6.2 %pair.12 = (bf16[256,3072]{1,0:T(8,128)(2,1)}, bf16[256,3072]{1,0:T(8,128)(2,1)}) custom-call(bf16[1,2,1024,3072]{3,2,1,0:T(8,128)(2,1)} %refs_0_.15, bf16[1,2,1024,3072]{3,2,1,0:T(8,128)(2,1)} %refs_1_.15, bf16[1,2,3072,1024]{3,2,1,0:T(8,128)(2,1)} %own.25), custom_call_target="tpu_custom_call" | custom-call | flops 786432 | bytes 7864320 | tf_op jit(solution)/shard_map/pair/pallas_call | solution.py:132
  37.0 46.7 %collective-permute-done.4.far = bf16[32,3072]{1,0:T(8,128)(2,1)} collective-permute-done((bf16[32,3072]{1,0:T(8,128)(2,1)S(1)}, bf16[32,3072]{1,0:T(8,128)(2,1)}, u32[]{:S(2)}, u32[]{:S(2)}) %collective-permute-start.4) | collective-permute-done | bytes 196640 | tf_op jit(solution)/shard_map/ppermute | solution.py:268
  83.6 2.0 collective-permute-start.11
  85.7 6.2 %pair.8 = (bf16[256,3072]{1,0:T(8,128)(2,1)}, bf16[256,3072]{1,0:T(8,128)(2,1)}) custom-call(bf16[1,2,1024,3072]{3,2,1,0:T(8,128)(2,1)} %refs_0_.15, bf16[1,2,1024,3072]{3,2,1,0:T(8,128)(2,1)} %refs_1_.15, bf16[1,2,3072,1024]{3,2,1,0:T(8,128)(2,1)} %own.25), custom_call_target="tpu_custom_call" | custom-call | flops 786432 | bytes 7864320 | tf_op jit(solution)/shard_map/pair/pallas_call | solution.py:132
  91.9 5.0 %pair.9 = (bf16[128,3072]{1,0:T(8,128)(2,1)}, bf16[32,3072]{1,0:T(8,128)(2,1)}, bf16[32,3072]{1,0:T(8,128)(2,1)}, bf16[64,3072]{1,0:T(8,128)(2,1)}, bf16[128,3072]{1,0:T(8,128)(2,1)}) custom-call(bf16[1,2,1024,3072]{3,2,1,0:T(8,128)(2,1)} %refs_0_.15, bf16[1,2,1024,3072]{3,2,1,0:T(8,128)(2,1)} %refs_1_.15, bf16[1,2,3072,1024]{3,2,1,0:T(8,128)(2,1)} %own.25), custom_call_target="tpu_custom_call" | custom-call | flops 393216 | bytes 3932160 | tf_op jit(solution)/shard_map/pair/pallas_call | solution.py:132
  96.9 2.0 collective-permute-start.1
  99.0 2.8 pair.10
  101.9 8.6 %adamw.20 = (bf16[768,1024]{1,0:T(8,128)(2,1)}, bf16[2,3072,1024]{2,1,0:T(8,128)(2,1)}, f32[2,768,1024]{2,1,0:T(8,128)}, f32[2,768,1024]{2,1,0:T(8,128)}) custom-call(s32[1]{0:T(128)} %bitcast.me, bf16[1,2,3072,1024]{3,2,1,0:T(8,128)(2,1)} %own.25, bf16[768,1024]{1,0:T(8,128)(2,1)} %get-tuple-element.113.near, ...), custom_call_target="tpu_custom_call" | custom-call | flops 11010048 | bytes 22020096 | tf_op jit(solution)/shard_map/adamw/pallas_call | solution.py:176
  110.5 6.1 %adamw.21 = (bf16[384,1024]{1,0:T(8,128)(2,1)}, bf16[2,3072,1024]{2,1,0:T(8,128)(2,1)}, f32[2,768,1024]{2,1,0:T(8,128)}, f32[2,768,1024]{2,1,0:T(8,128)}) custom-call(s32[1]{0:T(128)} %bitcast.me, bf16[1,2,3072,1024]{3,2,1,0:T(8,128)(2,1)} %own.25, ...), custom_call_target="tpu_custom_call", output_to_operand_aliasing={{1}: (7, {}), {2}: (8, {}), {3}: (9, {})} | custom-call | flops 5505024 | bytes 11010048 | tf_op jit(solution)/shard_map/adamw/pallas_call | solution.py:176
  116.6 3.8 adamw.22
  120.4 2.8 adamw.23
  123.2 2.2 adamw.24
  125.3 2.2 adamw.25
  127.6 86.1 %collective-permute-done.2.far = bf16[64,3072]{1,0:T(8,128)(2,1)} collective-permute-done((bf16[64,3072]{1,0:T(8,128)(2,1)}, bf16[64,3072]{1,0:T(8,128)(2,1)}, u32[]{:S(2)}, u32[]{:S(2)}) %collective-permute-start.2) | collective-permute-done | bytes 393248 | tf_op jit(solution)/shard_map/ppermute | solution.py:268
  213.7 0.5 collective-permute-start.27
  214.2 1.7 collective-permute-start.23
  216.3 1.7 collective-permute-start.33
  218.3 1.7 collective-permute-done.23.refs_2_
  220.0 22.3 %collective-permute-done.21.refs_0_ = bf16[48,1024]{1,0:T(8,128)(2,1)S(1)} collective-permute-done((bf16[48,1024]{1,0:T(8,128)(2,1)S(1)}, bf16[48,1024]{1,0:T(8,128)(2,1)S(1)}, u32[]{:S(2)}, u32[]{:S(2)}) %collective-permute-start.21) | collective-permute-done | bytes 98336 | tf_op jit(solution)/shard_map/ppermute | solution.py:268
  242.3 1.7 collective-permute-start.30
  244.1 2.8 adamw.13
  246.9 2.8 adamw.14
  249.6 3.8 adamw.15
  253.4 6.1 %adamw.16 = (bf16[256,3072]{1,0:T(8,128)(2,1)}, bf16[2,1024,3072]{2,1,0:T(8,128)(2,1)}, f32[2,256,3072]{2,1,0:T(8,128)}, f32[2,256,3072]{2,1,0:T(8,128)}) custom-call(s32[1]{0:T(128)} %bitcast.me, bf16[1,2,1024,3072]{3,2,1,0:T(8,128)(2,1)} %refs_0_.15, ...), custom_call_target="tpu_custom_call", output_to_operand_aliasing={{0}: (7, {}), {1}: (8, {}), {2}: (9, {}), {3}: (10, {})} | custom-call | flops 5505024 | bytes 11010048 | tf_op jit(solution)/shard_map/adamw/pallas_call | solution.py:176
  259.6 0.5 collective-permute-start.29
  260.4 1.3 collective-permute-done.29.beside
  262.0 0.4 copy-done.8
  262.8 0.9 collective-permute-start.36
  263.8 8.1 %adamw.18 = (bf16[256,3072]{1,0:T(8,128)(2,1)}, bf16[2,1024,3072]{2,1,0:T(8,128)(2,1)}, f32[2,256,3072]{2,1,0:T(8,128)}, f32[2,256,3072]{2,1,0:T(8,128)}) custom-call(s32[1]{0:T(128)} %bitcast.me, bf16[1,2,1024,3072]{3,2,1,0:T(8,128)(2,1)} %refs_1_.15, bf16[256,3072]{1,0:T(8,128)(2,1)} %get-tuple-element.103.near, bf16[256,3072]{1,0:T(8,128)(2,1)} %copy-done.1, ...), custom_call_target="tpu_custom_call" | custom-call | flops 11010048 | bytes 22020096 | tf_op jit(solution)/shard_map/adamw/pallas_call | solution.py:176
  271.9 1.1 collective-permute-start.17
  273.0 24.5 %collective-permute-done.9.across = bf16[256,3072]{1,0:T(8,128)(2,1)S(1)} collective-permute-done((bf16[256,3072]{1,0:T(8,128)(2,1)}, bf16[256,3072]{1,0:T(8,128)(2,1)S(1)}, u32[]{:S(2)}, u32[]{:S(2)}) %collective-permute-start.9) | collective-permute-done | bytes 1572896 | tf_op jit(solution)/shard_map/ppermute | solution.py:268
  297.6 0.5 collective-permute-start.16
  298.1 8.2 %adamw.19 = (bf16[256,3072]{1,0:T(8,128)(2,1)}, bf16[2,1024,3072]{2,1,0:T(8,128)(2,1)}, f32[2,256,3072]{2,1,0:T(8,128)}, f32[2,256,3072]{2,1,0:T(8,128)}) custom-call(s32[1]{0:T(128)} %bitcast.me, bf16[1,2,1024,3072]{3,2,1,0:T(8,128)(2,1)} %refs_1_.15, ...), custom_call_target="tpu_custom_call", output_to_operand_aliasing={{1}: (7, {}), {2}: (8, {}), {3}: (9, {})} | custom-call | flops 11010048 | bytes 22020096 | tf_op jit(solution)/shard_map/adamw/pallas_call | solution.py:176
  306.2 8.2 %adamw.17 = (bf16[256,3072]{1,0:T(8,128)(2,1)}, bf16[2,1024,3072]{2,1,0:T(8,128)(2,1)}, f32[2,256,3072]{2,1,0:T(8,128)}, f32[2,256,3072]{2,1,0:T(8,128)}) custom-call(s32[1]{0:T(128)} %bitcast.me, bf16[1,2,1024,3072]{3,2,1,0:T(8,128)(2,1)} %refs_0_.15, ...), custom_call_target="tpu_custom_call", output_to_operand_aliasing={{1}: (7, {}), {2}: (8, {}), {3}: (9, {})} | custom-call | flops 11010048 | bytes 22020096 | tf_op jit(solution)/shard_map/adamw/pallas_call | solution.py:176
  314.4 16.9 %collective-permute-done.36.across = bf16[768,1024]{1,0:T(8,128)(2,1)} collective-permute-done((bf16[768,1024]{1,0:T(8,128)(2,1)}, bf16[768,1024]{1,0:T(8,128)(2,1)}, u32[]{:S(2)}, u32[]{:S(2)}) %collective-permute-start.36) | collective-permute-done | bytes 1572896 | tf_op jit(solution)/shard_map/ppermute | solution.py:268
  331.6 1.7 collective-permute-start.6
  333.4 31.6 %collective-permute-done.17.across = bf16[256,3072]{1,0:T(8,128)(2,1)} collective-permute-done((bf16[256,3072]{1,0:T(8,128)(2,1)}, bf16[256,3072]{1,0:T(8,128)(2,1)}, u32[]{:S(2)}, u32[]{:S(2)}) %collective-permute-start.17) | collective-permute-done | bytes 1572896 | tf_op jit(solution)/shard_map/ppermute | solution.py:268
  365.1 0.5 collective-permute-start.18
  365.6 33.2 %collective-permute-done.14.across = bf16[256,3072]{1,0:T(8,128)(2,1)} collective-permute-done((bf16[256,3072]{1,0:T(8,128)(2,1)}, bf16[256,3072]{1,0:T(8,128)(2,1)}, u32[]{:S(2)}, u32[]{:S(2)}) %collective-permute-start.14) | collective-permute-done | bytes 1572896 | tf_op jit(solution)/shard_map/ppermute | solution.py:268
  398.8 32.8 %collective-permute-done.6.across = bf16[256,3072]{1,0:T(8,128)(2,1)} collective-permute-done((bf16[256,3072]{1,0:T(8,128)(2,1)}, bf16[256,3072]{1,0:T(8,128)(2,1)}, u32[]{:S(2)}, u32[]{:S(2)}) %collective-permute-start.6) | collective-permute-done | bytes 1572896 | tf_op jit(solution)/shard_map/ppermute | solution.py:268
  431.6 0.5 collective-permute-start.5
  432.1 0.6 copy-done.4
  432.7 0.6 copy-done.6
  433.3 1.1 copy-done.5
  434.4 0.5 collective-permute-start.38
  434.9 3.6 carry.11.before
  438.6 2.6 carry.12.before
  441.2 2.1 carry.13.refs_5_
  443.2 0.9 place.2.refs_3_
  444.2 3.6 carry.7.before
  447.8 0.7 place.3
  448.6 3.6 carry.9.before
  452.2 3.6 carry.10
  455.9 0.7 bitcast_dynamic-update-slice_fusion
  456.6 1.2 copy-done.3
  457.8 3.6 carry.8
  (72 shorter events, 2.4 us)
Async XLA Ops:
  7.3 89.7 %collective-permute-start.20 = (bf16[768,1024]{1,0:T(8,128)(2,1)}, bf16[768,1024]{1,0:T(8,128)(2,1)}, u32[]{:S(2)}, u32[]{:S(2)}) collective-permute-start(bf16[768,1024]{1,0:T(8,128)(2,1)} %get-tuple-element.114), channel_id=1, source_target_pairs={{0,2},{2,0},{1,3},{3,1},{4,6},{6,4},{5,7},{7,5}} | collective-permute-start | bytes 4718600 | tf_op jit(solution)/shard_map/ppermute | solution.py:268
  16.3 85.5 %collective-permute-start.19 = (bf16[768,1024]{1,0:T(8,128)(2,1)}, bf16[768,1024]{1,0:T(8,128)(2,1)S(1)}, u32[]{:S(2)}, u32[]{:S(2)}) collective-permute-start(bf16[768,1024]{1,0:T(8,128)(2,1)} %get-tuple-element.112), channel_id=1, source_target_pairs={{0,2},{2,0},{1,3},{3,1},{4,6},{6,4},{5,7},{7,5}} | collective-permute-start | bytes 4718600 | tf_op jit(solution)/shard_map/ppermute | solution.py:268
  18.1 65.5 %collective-permute-start.4 = (bf16[32,3072]{1,0:T(8,128)(2,1)S(1)}, bf16[32,3072]{1,0:T(8,128)(2,1)}, u32[]{:S(2)}, u32[]{:S(2)}) collective-permute-start(bf16[32,3072]{1,0:T(8,128)(2,1)S(1)} %first_pair.1), channel_id=1, source_target_pairs={{0,2},{2,0},{1,3},{3,1},{4,6},{6,4},{5,7},{7,5}} | collective-permute-start | bytes 589832 | tf_op jit(solution)/shard_map/ppermute | solution.py:268
  22.6 69.3 %collective-permute-start.3 = (bf16[32,3072]{1,0:T(8,128)(2,1)}, bf16[32,3072]{1,0:T(8,128)(2,1)S(1)}, u32[]{:S(2)}, u32[]{:S(2)}) collective-permute-start(bf16[32,3072]{1,0:T(8,128)(2,1)} %pair.11), channel_id=1, source_target_pairs={{0,2},{2,0},{1,3},{3,1},{4,6},{6,4},{5,7},{7,5}} | collective-permute-start | bytes 589832 | tf_op jit(solution)/shard_map/ppermute | solution.py:268
  28.8 185.4 %collective-permute-start.12 = (bf16[256,3072]{1,0:T(8,128)(2,1)}, bf16[256,3072]{1,0:T(8,128)(2,1)S(1)}, u32[]{:S(2)}, u32[]{:S(2)}) collective-permute-start(bf16[256,3072]{1,0:T(8,128)(2,1)} %get-tuple-element.104), channel_id=1, source_target_pairs={{0,2},{2,0},{1,3},{3,1},{4,6},{6,4},{5,7},{7,5}} | collective-permute-start | bytes 4718600 | tf_op jit(solution)/shard_map/ppermute | solution.py:268
  83.6 132.3 %collective-permute-start.11 = (bf16[256,3072]{1,0:T(8,128)(2,1)}, bf16[256,3072]{1,0:T(8,128)(2,1)}, u32[]{:S(2)}, u32[]{:S(2)}) collective-permute-start(bf16[256,3072]{1,0:T(8,128)(2,1)} %get-tuple-element.102), channel_id=1, source_target_pairs={{0,2},{2,0},{1,3},{3,1},{4,6},{6,4},{5,7},{7,5}} | collective-permute-start | bytes 4718600 | tf_op jit(solution)/shard_map/ppermute | solution.py:268
  91.8 5.1 %copy-start.10 = (bf16[32,3072]{1,0:T(8,128)(2,1)}, bf16[32,3072]{1,0:T(8,128)(2,1)S(1)}, u32[]{:S(2)}) copy-start(bf16[32,3072]{1,0:T(8,128)(2,1)S(1)} %collective-permute-done.3.far) | copy-start | bytes 589828
  91.8 124.4 %collective-permute-start = (bf16[256,3072]{1,0:T(8,128)(2,1)}, bf16[256,3072]{1,0:T(8,128)(2,1)}, u32[]{:S(2)}, u32[]{:S(2)}) collective-permute-start(bf16[256,3072]{1,0:T(8,128)(2,1)} %get-tuple-element.77), channel_id=1, source_target_pairs={{0,2},{2,0},{1,3},{3,1},{4,6},{6,4},{5,7},{7,5}} | collective-permute-start | bytes 4718600 | tf_op jit(solution)/shard_map/ppermute | solution.py:268
  96.9 116.8 %collective-permute-start.1 = (bf16[128,3072]{1,0:T(8,128)(2,1)}, bf16[128,3072]{1,0:T(8,128)(2,1)}, u32[]{:S(2)}, u32[]{:S(2)}) collective-permute-start(bf16[128,3072]{1,0:T(8,128)(2,1)} %get-tuple-element.79), channel_id=1, source_target_pairs={{0,2},{2,0},{1,3},{3,1},{4,6},{6,4},{5,7},{7,5}} | collective-permute-start | bytes 2359304 | tf_op jit(solution)/shard_map/ppermute | solution.py:268
  101.8 8.7 %copy-start = (bf16[768,1024]{1,0:T(8,128)(2,1)}, bf16[768,1024]{1,0:T(8,128)(2,1)S(1)}, u32[]{:S(2)}) copy-start(bf16[768,1024]{1,0:T(8,128)(2,1)S(1)} %collective-permute-done.19.far) | copy-start | bytes 4718596
  101.8 111.9 %collective-permute-start.2 = (bf16[64,3072]{1,0:T(8,128)(2,1)}, bf16[64,3072]{1,0:T(8,128)(2,1)}, u32[]{:S(2)}, u32[]{:S(2)}) collective-permute-start(bf16[64,3072]{1,0:T(8,128)(2,1)} %pair.10), channel_id=1, source_target_pairs={{0,2},{2,0},{1,3},{3,1},{4,6},{6,4},{5,7},{7,5}} | collective-permute-start | bytes 1179656 | tf_op jit(solution)/shard_map/ppermute | solution.py:268
  125.3 88.4 %copy-start.12 = (bf16[48,1024]{1,0:T(8,128)(2,1)S(1)}, bf16[48,1024]{1,0:T(8,128)(2,1)}, u32[]{:S(2)}) copy-start(bf16[48,1024]{1,0:T(8,128)(2,1)} %get-tuple-element.127) | copy-start | bytes 294916
  125.3 90.6 %copy-start.11 = (bf16[96,1024]{1,0:T(8,128)(2,1)S(1)}, bf16[96,1024]{1,0:T(8,128)(2,1)}, u32[]{:S(2)}) copy-start(bf16[96,1024]{1,0:T(8,128)(2,1)} %get-tuple-element.132) | copy-start | bytes 589828
  213.7 4.3 collective-permute-start.28
  213.7 4.3 collective-permute-start.27
  214.2 32.6 %copy-start.1 = (bf16[256,3072]{1,0:T(8,128)(2,1)}, bf16[256,3072]{1,0:T(8,128)(2,1)S(1)}, u32[]{:S(2)}) copy-start(bf16[256,3072]{1,0:T(8,128)(2,1)S(1)} %collective-permute-done.12.far) | copy-start | bytes 4718596
  214.2 5.8 %collective-permute-start.23 = (bf16[48,1024]{1,0:T(8,128)(2,1)}, bf16[48,1024]{1,0:T(8,128)(2,1)S(1)}, u32[]{:S(2)}, u32[]{:S(2)}) collective-permute-start(bf16[48,1024]{1,0:T(8,128)(2,1)} %get-tuple-element.131), channel_id=1, source_target_pairs={{0,2},{2,0},{1,3},{3,1},{4,6},{6,4},{5,7},{7,5}} | collective-permute-start | bytes 294920 | tf_op jit(solution)/shard_map/ppermute | solution.py:268
  216.0 28.1 %collective-permute-start.25 = (bf16[96,1024]{1,0:T(8,128)(2,1)S(1)}, bf16[96,1024]{1,0:T(8,128)(2,1)S(1)}, u32[]{:S(2)}, u32[]{:S(2)}) collective-permute-start(bf16[96,1024]{1,0:T(8,128)(2,1)S(1)} %copy-done.11), channel_id=1, source_target_pairs={{0,2},{2,0},{1,3},{3,1},{4,6},{6,4},{5,7},{7,5}} | collective-permute-start | bytes 589832 | tf_op jit(solution)/shard_map/ppermute | solution.py:268
  216.3 46.5 %collective-permute-start.33 = (bf16[384,1024]{1,0:T(8,128)(2,1)}, bf16[384,1024]{1,0:T(8,128)(2,1)}, u32[]{:S(2)}, u32[]{:S(2)}) collective-permute-start(bf16[384,1024]{1,0:T(8,128)(2,1)} %get-tuple-element.134), channel_id=1, source_target_pairs={{0,2},{2,0},{1,3},{3,1},{4,6},{6,4},{5,7},{7,5}} | collective-permute-start | bytes 2359304 | tf_op jit(solution)/shard_map/ppermute | solution.py:268
  218.0 45.7 %collective-permute-start.32 = (bf16[384,1024]{1,0:T(8,128)(2,1)}, bf16[384,1024]{1,0:T(8,128)(2,1)}, u32[]{:S(2)}, u32[]{:S(2)}) collective-permute-start(bf16[384,1024]{1,0:T(8,128)(2,1)} %get-tuple-element.134), channel_id=1, source_target_pairs={{0,1},{1,0},{2,3},{3,2},{4,5},{5,4},{6,7},{7,6}} | collective-permute-start | bytes 2359304 | tf_op jit(solution)/shard_map/ppermute | solution.py:268
  218.0 24.3 %collective-permute-start.21 = (bf16[48,1024]{1,0:T(8,128)(2,1)S(1)}, bf16[48,1024]{1,0:T(8,128)(2,1)S(1)}, u32[]{:S(2)}, u32[]{:S(2)}) collective-permute-start(bf16[48,1024]{1,0:T(8,128)(2,1)S(1)} %copy-done.12), channel_id=1, source_target_pairs={{0,2},{2,0},{1,3},{3,1},{4,6},{6,4},{5,7},{7,5}} | collective-permute-start | bytes 294920 | tf_op jit(solution)/shard_map/ppermute | solution.py:268
  220.0 39.5 %collective-permute-start.24 = (bf16[96,1024]{1,0:T(8,128)(2,1)S(1)}, bf16[96,1024]{1,0:T(8,128)(2,1)S(1)}, u32[]{:S(2)}, u32[]{:S(2)}) collective-permute-start(bf16[96,1024]{1,0:T(8,128)(2,1)S(1)} %copy-done.11), channel_id=1, source_target_pairs={{0,1},{1,0},{2,3},{3,2},{4,5},{5,4},{6,7},{7,6}} | collective-permute-start | bytes 589832 | tf_op jit(solution)/shard_map/ppermute | solution.py:268
  242.3 18.0 %collective-permute-start.30 = (bf16[192,1024]{1,0:T(8,128)(2,1)}, bf16[192,1024]{1,0:T(8,128)(2,1)}, u32[]{:S(2)}, u32[]{:S(2)}) collective-permute-start(bf16[192,1024]{1,0:T(8,128)(2,1)} %get-tuple-element.133), channel_id=1, source_target_pairs={{0,2},{2,0},{1,3},{3,1},{4,6},{6,4},{5,7},{7,5}} | collective-permute-start | bytes 1179656 | tf_op jit(solution)/shard_map/ppermute | solution.py:268
  244.1 16.0 %collective-permute-start.22 = (bf16[48,1024]{1,0:T(8,128)(2,1)S(1)}, bf16[48,1024]{1,0:T(8,128)(2,1)S(1)}, u32[]{:S(2)}, u32[]{:S(2)}) collective-permute-start(bf16[48,1024]{1,0:T(8,128)(2,1)S(1)} %collective-permute-done.21.refs_0_), channel_id=1, source_target_pairs={{0,1},{1,0},{2,3},{3,2},{4,5},{5,4},{6,7},{7,6}} | collective-permute-start | bytes 294920 | tf_op jit(solution)/shard_map/ppermute | solution.py:268
  259.6 2.1 collective-permute-start.29
  260.1 37.5 %collective-permute-start.9 = (bf16[256,3072]{1,0:T(8,128)(2,1)}, bf16[256,3072]{1,0:T(8,128)(2,1)S(1)}, u32[]{:S(2)}, u32[]{:S(2)}) collective-permute-start(bf16[256,3072]{1,0:T(8,128)(2,1)} %get-tuple-element.99), channel_id=1, source_target_pairs={{0,2},{2,0},{1,3},{3,1},{4,6},{6,4},{5,7},{7,5}} | collective-permute-start | bytes 4718600 | tf_op jit(solution)/shard_map/ppermute | solution.py:268
  260.4 1.6 collective-permute-start.26
  261.6 0.8 copy-start.8
  261.6 10.3 %collective-permute-start.31 = (bf16[192,1024]{1,0:T(8,128)(2,1)}, bf16[192,1024]{1,0:T(8,128)(2,1)S(1)}, u32[]{:S(2)}, u32[]{:S(2)}) collective-permute-start(bf16[192,1024]{1,0:T(8,128)(2,1)} %collective-permute-done.30.across), channel_id=1, source_target_pairs={{0,1},{1,0},{2,3},{3,2},{4,5},{5,4},{6,7},{7,6}} | collective-permute-start | bytes 1179656 | tf_op jit(solution)/shard_map/ppermute | solution.py:268
  262.4 35.2 %collective-permute-start.8 = (bf16[256,3072]{1,0:T(8,128)(2,1)}, bf16[256,3072]{1,0:T(8,128)(2,1)}, u32[]{:S(2)}, u32[]{:S(2)}) collective-permute-start(bf16[256,3072]{1,0:T(8,128)(2,1)} %get-tuple-element.99), channel_id=1, source_target_pairs={{0,1},{1,0},{2,3},{3,2},{4,5},{5,4},{6,7},{7,6}} | collective-permute-start | bytes 4718600 | tf_op jit(solution)/shard_map/ppermute | solution.py:268
  262.8 68.6 %collective-permute-start.36 = (bf16[768,1024]{1,0:T(8,128)(2,1)}, bf16[768,1024]{1,0:T(8,128)(2,1)}, u32[]{:S(2)}, u32[]{:S(2)}) collective-permute-start(bf16[768,1024]{1,0:T(8,128)(2,1)} %get-tuple-element.135), channel_id=1, source_target_pairs={{0,2},{2,0},{1,3},{3,1},{4,6},{6,4},{5,7},{7,5}} | collective-permute-start | bytes 4718600 | tf_op jit(solution)/shard_map/ppermute | solution.py:268
  263.7 68.0 %collective-permute-start.35 = (bf16[768,1024]{1,0:T(8,128)(2,1)}, bf16[768,1024]{1,0:T(8,128)(2,1)}, u32[]{:S(2)}, u32[]{:S(2)}) collective-permute-start(bf16[768,1024]{1,0:T(8,128)(2,1)} %get-tuple-element.135), channel_id=1, source_target_pairs={{0,1},{1,0},{2,3},{3,2},{4,5},{5,4},{6,7},{7,6}} | collective-permute-start | bytes 4718600 | tf_op jit(solution)/shard_map/ppermute | solution.py:268
  271.9 1.1 copy-start.9
  271.9 93.1 %collective-permute-start.17 = (bf16[256,3072]{1,0:T(8,128)(2,1)}, bf16[256,3072]{1,0:T(8,128)(2,1)}, u32[]{:S(2)}, u32[]{:S(2)}) collective-permute-start(bf16[256,3072]{1,0:T(8,128)(2,1)} %get-tuple-element.109), channel_id=1, source_target_pairs={{0,2},{2,0},{1,3},{3,1},{4,6},{6,4},{5,7},{7,5}} | collective-permute-start | bytes 4718600 | tf_op jit(solution)/shard_map/ppermute | solution.py:268
  297.5 35.8 %copy-start.2 = (bf16[256,3072]{1,0:T(8,128)(2,1)}, bf16[256,3072]{1,0:T(8,128)(2,1)S(1)}, u32[]{:S(2)}) copy-start(bf16[256,3072]{1,0:T(8,128)(2,1)S(1)} %collective-permute-done.9.across) | copy-start | bytes 4718596
  297.5 35.8 %collective-permute-start.34 = (bf16[384,1024]{1,0:T(8,128)(2,1)}, bf16[384,1024]{1,0:T(8,128)(2,1)S(1)}, u32[]{:S(2)}, u32[]{:S(2)}) collective-permute-start(bf16[384,1024]{1,0:T(8,128)(2,1)} %collective-permute-done.33.across), channel_id=1, source_target_pairs={{0,1},{1,0},{2,3},{3,2},{4,5},{5,4},{6,7},{7,6}} | collective-permute-start | bytes 2359304 | tf_op jit(solution)/shard_map/ppermute | solution.py:268
  297.6 67.5 %collective-permute-start.16 = (bf16[256,3072]{1,0:T(8,128)(2,1)}, bf16[256,3072]{1,0:T(8,128)(2,1)}, u32[]{:S(2)}, u32[]{:S(2)}) collective-permute-start(bf16[256,3072]{1,0:T(8,128)(2,1)} %get-tuple-element.109), channel_id=1, source_target_pairs={{0,1},{1,0},{2,3},{3,2},{4,5},{5,4},{6,7},{7,6}} | collective-permute-start | bytes 4718600 | tf_op jit(solution)/shard_map/ppermute | solution.py:268
  331.4 67.4 %collective-permute-start.14 = (bf16[256,3072]{1,0:T(8,128)(2,1)}, bf16[256,3072]{1,0:T(8,128)(2,1)}, u32[]{:S(2)}, u32[]{:S(2)}) collective-permute-start(bf16[256,3072]{1,0:T(8,128)(2,1)} %get-tuple-element.108), channel_id=1, source_target_pairs={{0,2},{2,0},{1,3},{3,1},{4,6},{6,4},{5,7},{7,5}} | collective-permute-start | bytes 4718600 | tf_op jit(solution)/shard_map/ppermute | solution.py:268
  331.6 99.9 %collective-permute-start.6 = (bf16[256,3072]{1,0:T(8,128)(2,1)}, bf16[256,3072]{1,0:T(8,128)(2,1)}, u32[]{:S(2)}, u32[]{:S(2)}) collective-permute-start(bf16[256,3072]{1,0:T(8,128)(2,1)} %get-tuple-element.98), channel_id=1, source_target_pairs={{0,2},{2,0},{1,3},{3,1},{4,6},{6,4},{5,7},{7,5}} | collective-permute-start | bytes 4718600 | tf_op jit(solution)/shard_map/ppermute | solution.py:268
  333.4 105.2 %copy-start.7 = (bf16[384,1024]{1,0:T(8,128)(2,1)}, bf16[384,1024]{1,0:T(8,128)(2,1)S(1)}, u32[]{:S(2)}) copy-start(bf16[384,1024]{1,0:T(8,128)(2,1)S(1)} %collective-permute-done.34.corner) | copy-start | bytes 2359300
  333.4 98.2 %collective-permute-start.10 = (bf16[256,3072]{1,0:T(8,128)(2,1)S(1)}, bf16[256,3072]{1,0:T(8,128)(2,1)S(1)}, u32[]{:S(2)}, u32[]{:S(2)}) collective-permute-start(bf16[256,3072]{1,0:T(8,128)(2,1)S(1)} %collective-permute-done.9.across), channel_id=1, source_target_pairs={{0,1},{1,0},{2,3},{3,2},{4,5},{5,4},{6,7},{7,6}} | collective-permute-start | bytes 4718600 | tf_op jit(solution)/shard_map/ppermute | solution.py:268
  365.1 67.0 %collective-permute-start.37 = (bf16[768,1024]{1,0:T(8,128)(2,1)}, bf16[768,1024]{1,0:T(8,128)(2,1)S(1)}, u32[]{:S(2)}, u32[]{:S(2)}) collective-permute-start(bf16[768,1024]{1,0:T(8,128)(2,1)} %collective-permute-done.36.across), channel_id=1, source_target_pairs={{0,1},{1,0},{2,3},{3,2},{4,5},{5,4},{6,7},{7,6}} | collective-permute-start | bytes 4718600 | tf_op jit(solution)/shard_map/ppermute | solution.py:268
  365.1 67.6 %collective-permute-start.18 = (bf16[256,3072]{1,0:T(8,128)(2,1)}, bf16[256,3072]{1,0:T(8,128)(2,1)S(1)}, u32[]{:S(2)}, u32[]{:S(2)}) collective-permute-start(bf16[256,3072]{1,0:T(8,128)(2,1)} %collective-permute-done.17.across), channel_id=1, source_target_pairs={{0,1},{1,0},{2,3},{3,2},{4,5},{5,4},{6,7},{7,6}} | collective-permute-start | bytes 4718600 | tf_op jit(solution)/shard_map/ppermute | solution.py:268
  398.8 53.5 %collective-permute-start.13 = (bf16[256,3072]{1,0:T(8,128)(2,1)}, bf16[256,3072]{1,0:T(8,128)(2,1)}, u32[]{:S(2)}, u32[]{:S(2)}) collective-permute-start(bf16[256,3072]{1,0:T(8,128)(2,1)} %get-tuple-element.108), channel_id=1, source_target_pairs={{0,1},{1,0},{2,3},{3,2},{4,5},{5,4},{6,7},{7,6}} | collective-permute-start | bytes 4718600 | tf_op jit(solution)/shard_map/ppermute | solution.py:268
  431.5 20.7 %collective-permute-start.15 = (bf16[256,3072]{1,0:T(8,128)(2,1)}, bf16[256,3072]{1,0:T(8,128)(2,1)}, u32[]{:S(2)}, u32[]{:S(2)}) collective-permute-start(bf16[256,3072]{1,0:T(8,128)(2,1)} %collective-permute-done.14.across), channel_id=1, source_target_pairs={{0,1},{1,0},{2,3},{3,2},{4,5},{5,4},{6,7},{7,6}} | collective-permute-start | bytes 4718600 | tf_op jit(solution)/shard_map/ppermute | solution.py:268
  431.5 1.2 copy-start.4
  431.6 25.0 %collective-permute-start.5 = (bf16[256,3072]{1,0:T(8,128)(2,1)}, bf16[256,3072]{1,0:T(8,128)(2,1)S(1)}, u32[]{:S(2)}, u32[]{:S(2)}) collective-permute-start(bf16[256,3072]{1,0:T(8,128)(2,1)} %get-tuple-element.98), channel_id=1, source_target_pairs={{0,1},{1,0},{2,3},{3,2},{4,5},{5,4},{6,7},{7,6}} | collective-permute-start | bytes 4718600 | tf_op jit(solution)/shard_map/ppermute | solution.py:268
  432.1 1.2 copy-start.6
  432.1 24.5 %collective-permute-start.7 = (bf16[256,3072]{1,0:T(8,128)(2,1)}, bf16[256,3072]{1,0:T(8,128)(2,1)}, u32[]{:S(2)}, u32[]{:S(2)}) collective-permute-start(bf16[256,3072]{1,0:T(8,128)(2,1)} %collective-permute-done.6.across), channel_id=1, source_target_pairs={{0,1},{1,0},{2,3},{3,2},{4,5},{5,4},{6,7},{7,6}} | collective-permute-start | bytes 4718600 | tf_op jit(solution)/shard_map/ppermute | solution.py:268
  433.3 1.1 copy-start.5
  434.4 21.5 %collective-permute-start.38 = (bf16[48,1024]{1,0:T(8,128)(2,1)S(1)}, bf16[48,1024]{1,0:T(8,128)(2,1)S(1)}, u32[]{:S(2)}, u32[]{:S(2)}) collective-permute-start(bf16[48,1024]{1,0:T(8,128)(2,1)S(1)} %collective-permute-done.23.refs_2_), channel_id=1, source_target_pairs={{0,1},{1,0},{2,3},{3,2},{4,5},{5,4},{6,7},{7,6}} | collective-permute-start | bytes 294920 | tf_op jit(solution)/shard_map/ppermute | solution.py:268
  456.6 1.2 copy-start.3
where the time goes:
time: 462 us
  waiting for transfers between devices  297 us (64%)
  Pallas kernels  133 us (29%)
  starting transfers between devices  25.2 us (5%)
    ppermute x39, waiting for transfers between devices, send(): return lax.ppermute(x, 'dp', to)  297 us
    pallas_call x13, Pallas kernels, adamw(): pl.pallas_call(functools.partial(adamw_body, len(have)), grid_spec=pltpu....  65.6 us
    pallas_call x8, Pallas kernels, pair(): pl.pallas_call(functools.partial(pair_body, chunk, nears), in_specs=[anyw...  41.6 us
    ppermute x39, starting transfers between devices, send(): return lax.ppermute(x, 'dp', to)  25.2 us
    pallas_call x7, Pallas kernels, carry(): pl.pallas_call(functools.partial(carry_body, chunk, block), in_specs=[pl....  22.8 us
  transfers between devices with their start and end apart: 39, of which 10 were waited for; matrix products, arithmetic and copies ran while one was open for 0% of the time, Pallas kernels for 27%

commit v1 on v0

--- a/solution.py
+++ b/solution.py
@@ -62,15 +62,16 @@
         for i, c in enumerate(nears)
     ]
     outs = [pltpu.make_async_copy(total.at[pl.ds(t * tile, tile)], both.at[pl.ds(t * tile, tile)], out_sem.at[t]) for t in range(count)]
+    for own in owns:
+        own.start()
     pl.semaphore_wait(barrier, 1)
-    for far, own in zip(fars, owns):
+    for far in fars:
         far.start()
-        own.start()
     for copy in beside:
         copy.start()
     for t in range(count):
+        fars[t].wait_recv()
         owns[t].wait()
-        fars[t].wait_recv()
         here = pl.ds(t * tile, tile)
         total[here] = (got[here].astype(jnp.float32) + mine[here].astype(jnp.float32)).astype(jnp.bfloat16)
         outs[t].start()
@@ -97,8 +98,8 @@
     own.start()
     pl.semaphore_wait(barrier, 1)
     far.start()
+    far.wait_recv()
     own.wait()
-    far.wait_recv()
     both[...] = (got[...].astype(jnp.float32) + mine[...].astype(jnp.float32)).astype(jnp.bfloat16)
     far.wait_send()
 
@@ -162,7 +163,7 @@
     _, layer, sum_first, _ = SUMS[r]
     _, _, chunk_first, chunk_rows = CHUNKS[c]
     block, cols = m.shape[1], m.shape[2]
-    tile = math.gcd(rows, first, block, first - sum_first, first - chunk_first, 128 * 3072 // cols)
+    tile = math.gcd(rows, first, block, first - sum_first, first - chunk_first, 64 * 3072 // cols)
     at, per = first // tile, block // tile
     of_sum, of_chunk = (first - sum_first) // tile, (first - chunk_first) // tile
     mine = pl.BlockSpec((1, tile, cols), lambda i, me: (layer, at + i, 0))
@@ -223,13 +224,15 @@
     )(me, *pieces, out)
 
 
-def carry_body(chunk, block, me, beside, across, corner, before, out, held, in_sem, out_sem):
-    _, layer, first, rows = chunk
-    ins = [pltpu.make_async_copy(src, held.at[i], in_sem.at[i]) for i, src in enumerate((beside, across, corner))]
-    outs = [
-        pltpu.make_async_copy(held.at[i], out.at[layer, pl.ds(pl.multiple_of((me[0] ^ (1 + i)) * block + first, 16), rows)], out_sem.at[i])
-        for i in range(3)
-    ]
+def carry_body(chunks, block, me, *refs):
+    n = 3 * len(chunks)
+    pieces, (_, out, held, in_sem, out_sem) = refs[:n], refs[n:]
+    ins, outs = [], []
+    for i, src in enumerate(pieces):
+        _, layer, first, rows = chunks[i // 3]
+        to = out.at[layer, pl.ds(pl.multiple_of((me[0] ^ (1 + i % 3)) * block + first, 16), rows)]
+        ins.append(pltpu.make_async_copy(src, held.at[i], in_sem.at[i]))
+        outs.append(pltpu.make_async_copy(held.at[i], to, out_sem.at[i]))
     for copy in ins:
         copy.start()
     for came, goes in zip(ins, outs):
@@ -239,22 +242,22 @@
         copy.wait()
 
 
-def carry(me, chunk, pieces, out, block):
-    _, _, _, rows = chunk
-    cols = out.shape[2]
+def carry(me, chunks, pieces, out, block):
+    rows, cols = pieces[0].shape
+    n = len(pieces)
     anywhere = pl.BlockSpec(memory_space=pl.ANY)
     return pl.pallas_call(
-        functools.partial(carry_body, chunk, block),
-        in_specs=[pl.BlockSpec(memory_space=pltpu.SMEM)] + [anywhere] * 4,
+        functools.partial(carry_body, chunks, block),
+        in_specs=[pl.BlockSpec(memory_space=pltpu.SMEM)] + [anywhere] * (n + 1),
         out_specs=anywhere,
         out_shape=jax.ShapeDtypeStruct(out.shape, out.dtype),
-        input_output_aliases={4: 0},
+        input_output_aliases={1 + n: 0},
         scratch_shapes=[
-            pltpu.VMEM((3, rows, cols), jnp.bfloat16),
-            pltpu.SemaphoreType.DMA((3,)),
-            pltpu.SemaphoreType.DMA((3,)),
+            pltpu.VMEM((n, rows, cols), jnp.bfloat16),
+            pltpu.SemaphoreType.DMA((n,)),
+            pltpu.SemaphoreType.DMA((n,)),
         ],
-        cost_estimate=pl.CostEstimate(flops=3 * rows * cols, bytes_accessed=12 * rows * cols, transcendentals=0),
+        cost_estimate=pl.CostEstimate(flops=n * rows * cols, bytes_accessed=4 * n * rows * cols, transcendentals=0),
         name="carry",
     )(me, *pieces, out)
 
@@ -294,9 +297,13 @@
                 what += ((LAST - 1, 1), (LAST, 1))
             if c == LAST - 1:
                 what = ((c, 2), (c, 3), (LAST, 2))
+            if c in (0, 2):
+                continue
+            if c in (1, 3):
+                what = ((c - 1, 1), (c - 1, 2), (c - 1, 3)) + what
             pieces = [came[other][i] for i, other in what]
             if c < LAST - 2:
-                state[which][0] = carry(me, CHUNKS[c], pieces, state[which][0], m[which].shape[1])
+                state[which][0] = carry(me, [CHUNKS[i] for i, _ in what[::3]], pieces, state[which][0], m[which].shape[1])
             else:
                 state[which][0] = place(me, what, pieces, state[which][0], m[which].shape[1])
         which, layer, first, _ = CHUNKS[LAST]

time: 462 us -> 450 us (0.974)
  waiting for transfers between devices: 297 us -> 284 us
    ppermute x39, waiting for transfers between devices: 297 us -> 284 us  [send(): return lax.ppermute(x, 'dp', to)]
    pallas_call x7 -> x5, Pallas kernels: 22.8 us -> 22.8 us  [carry(): pl.pallas_call(functools.partial(carry_body, chunks, block), in_specs=[pl...]
  transfers between devices with their start and end apart: 39 -> 39, of which waited for: 10 -> 12; matrix products, arithmetic and copies ran while one was open for 0% -> 0% of each run, Pallas kernels for 27% -> 27%
where the time goes in v1:
time: 450 us
  waiting for transfers between devices  284 us (63%)
  Pallas kernels  135 us (30%)
  starting transfers between devices  26.7 us (6%)
    ppermute x39, waiting for transfers between devices, send(): return lax.ppermute(x, 'dp', to)  284 us
    pallas_call x13, Pallas kernels, adamw(): pl.pallas_call(functools.partial(adamw_body, len(have)), grid_spec=pltpu....  67.1 us
    pallas_call x8, Pallas kernels, pair(): pl.pallas_call(functools.partial(pair_body, chunk, nears), in_specs=[anyw...  41.6 us
    ppermute x39, starting transfers between devices, send(): return lax.ppermute(x, 'dp', to)  26.7 us
    pallas_call x5, Pallas kernels, carry(): pl.pallas_call(functools.partial(carry_body, chunks, block), in_specs=[pl...  22.8 us
  transfers between devices with their start and end apart: 39, of which 12 were waited for; matrix products, arithmetic and copies ran while one was open for 0% of the time, Pallas kernels for 27%

profile of v1, /device:TPU:0, one launch (start us, length us, event | category | flops | bytes accessed | tf_op | source)
XLA Modules:
  0.0 449.9 jit_solution(11541691031754712712)
XLA Ops:
  0.6 6.6 %pair.15 = (bf16[768,1024]{1,0:T(8,128)(2,1)}, bf16[768,1024]{1,0:T(8,128)(2,1)}) custom-call(bf16[1,2,1024,3072]{3,2,1,0:T(8,128)(2,1)} %refs_0_.15, bf16[1,2,1024,3072]{3,2,1,0:T(8,128)(2,1)} %refs_1_.15, bf16[1,2,3072,1024]{3,2,1,0:T(8,128)(2,1)} %own.25), custom_call_target="tpu_custom_call" | custom-call | flops 786432 | bytes 7864320 | tf_op jit(solution)/shard_map/pair/pallas_call | solution.py:133
  7.3 2.9 collective-permute-start.20
  10.2 6.2 %pair.14 = (bf16[768,1024]{1,0:T(8,128)(2,1)}, bf16[768,1024]{1,0:T(8,128)(2,1)}) custom-call(bf16[1,2,1024,3072]{3,2,1,0:T(8,128)(2,1)} %refs_0_.15, bf16[1,2,1024,3072]{3,2,1,0:T(8,128)(2,1)} %refs_1_.15, bf16[1,2,3072,1024]{3,2,1,0:T(8,128)(2,1)} %own.25), custom_call_target="tpu_custom_call" | custom-call | flops 786432 | bytes 7864320 | tf_op jit(solution)/shard_map/pair/pallas_call | solution.py:133
  16.4 1.7 first_pair.1
  18.1 2.0 collective-permute-start.3
  20.1 2.4 pair.10
  22.6 6.2 %pair.12 = (bf16[256,3072]{1,0:T(8,128)(2,1)}, bf16[256,3072]{1,0:T(8,128)(2,1)}) custom-call(bf16[1,2,1024,3072]{3,2,1,0:T(8,128)(2,1)} %refs_0_.15, bf16[1,2,1024,3072]{3,2,1,0:T(8,128)(2,1)} %refs_1_.15, bf16[1,2,3072,1024]{3,2,1,0:T(8,128)(2,1)} %own.25), custom_call_target="tpu_custom_call" | custom-call | flops 786432 | bytes 7864320 | tf_op jit(solution)/shard_map/pair/pallas_call | solution.py:133
  28.8 2.0 collective-permute-start.11
  30.8 6.2 %pair.13 = (bf16[256,3072]{1,0:T(8,128)(2,1)}, bf16[256,3072]{1,0:T(8,128)(2,1)}) custom-call(bf16[1,2,1024,3072]{3,2,1,0:T(8,128)(2,1)} %refs_0_.15, bf16[1,2,1024,3072]{3,2,1,0:T(8,128)(2,1)} %refs_1_.15, bf16[1,2,3072,1024]{3,2,1,0:T(8,128)(2,1)} %own.25), custom_call_target="tpu_custom_call" | custom-call | flops 786432 | bytes 7864320 | tf_op jit(solution)/shard_map/pair/pallas_call | solution.py:133
  37.0 6.2 %pair.11 = (bf16[256,3072]{1,0:T(8,128)(2,1)}, bf16[256,3072]{1,0:T(8,128)(2,1)}) custom-call(bf16[1,2,1024,3072]{3,2,1,0:T(8,128)(2,1)} %refs_0_.15, bf16[1,2,1024,3072]{3,2,1,0:T(8,128)(2,1)} %refs_1_.15, bf16[1,2,3072,1024]{3,2,1,0:T(8,128)(2,1)} %own.25), custom_call_target="tpu_custom_call" | custom-call | flops 786432 | bytes 7864320 | tf_op jit(solution)/shard_map/pair/pallas_call | solution.py:133
  43.2 40.5 %collective-permute-done.3.far = bf16[32,3072]{1,0:T(8,128)(2,1)} collective-permute-done((bf16[32,3072]{1,0:T(8,128)(2,1)S(1)}, bf16[32,3072]{1,0:T(8,128)(2,1)}, u32[]{:S(2)}, u32[]{:S(2)}) %collective-permute-start.3) | collective-permute-done | bytes 196640 | tf_op jit(solution)/shard_map/ppermute | solution.py:271
  83.6 2.0 collective-permute-start.15
  85.7 2.1 collective-permute-done.2.far
  87.7 2.0 collective-permute-start.7
  89.8 5.0 %pair.8 = (bf16[128,3072]{1,0:T(8,128)(2,1)}, bf16[32,3072]{1,0:T(8,128)(2,1)}, bf16[32,3072]{1,0:T(8,128)(2,1)}, bf16[64,3072]{1,0:T(8,128)(2,1)}, bf16[128,3072]{1,0:T(8,128)(2,1)}) custom-call(bf16[1,2,1024,3072]{3,2,1,0:T(8,128)(2,1)} %refs_0_.15, bf16[1,2,1024,3072]{3,2,1,0:T(8,128)(2,1)} %refs_1_.15, bf16[1,2,3072,1024]{3,2,1,0:T(8,128)(2,1)} %own.25), custom_call_target="tpu_custom_call" | custom-call | flops 393216 | bytes 3932160 | tf_op jit(solution)/shard_map/pair/pallas_call | solution.py:133
  94.9 2.8 pair.9
  97.7 2.0 collective-permute-start.1
  99.7 9.2 %adamw.20 = (bf16[768,1024]{1,0:T(8,128)(2,1)}, bf16[2,3072,1024]{2,1,0:T(8,128)(2,1)}, f32[2,768,1024]{2,1,0:T(8,128)}, f32[2,768,1024]{2,1,0:T(8,128)}) custom-call(s32[1]{0:T(128)} %bitcast.me, bf16[1,2,3072,1024]{3,2,1,0:T(8,128)(2,1)} %own.25, bf16[768,1024]{1,0:T(8,128)(2,1)} %get-tuple-element.113.near, ...), custom_call_target="tpu_custom_call" | custom-call | flops 11010048 | bytes 22020096 | tf_op jit(solution)/shard_map/adamw/pallas_call | solution.py:177
  108.9 4.9 %adamw.21 = (bf16[384,1024]{1,0:T(8,128)(2,1)}, bf16[2,3072,1024]{2,1,0:T(8,128)(2,1)}, f32[2,768,1024]{2,1,0:T(8,128)}, f32[2,768,1024]{2,1,0:T(8,128)}) custom-call(s32[1]{0:T(128)} %bitcast.me, bf16[1,2,3072,1024]{3,2,1,0:T(8,128)(2,1)} %own.25, ...), custom_call_target="tpu_custom_call", output_to_operand_aliasing={{1}: (7, {}), {2}: (8, {}), {3}: (9, {})} | custom-call | flops 5505024 | bytes 11010048 | tf_op jit(solution)/shard_map/adamw/pallas_call | solution.py:177
  113.9 3.8 adamw.22
  117.7 2.8 adamw.23
  120.4 2.2 adamw.24
  122.6 2.2 adamw.25
  124.8 88.9 %collective-permute-done.1.far = bf16[64,3072]{1,0:T(8,128)(2,1)} collective-permute-done((bf16[64,3072]{1,0:T(8,128)(2,1)}, bf16[64,3072]{1,0:T(8,128)(2,1)}, u32[]{:S(2)}, u32[]{:S(2)}) %collective-permute-start.1) | collective-permute-done | bytes 393248 | tf_op jit(solution)/shard_map/ppermute | solution.py:271
  213.7 0.5 collective-permute-start.27
  214.2 1.8 collective-permute-start.25
  216.0 0.3 collective-permute-start.21
  216.3 1.7 collective-permute-start.30
  218.3 5.8 %collective-permute-done.21.refs_0_ = bf16[48,1024]{1,0:T(8,128)(2,1)S(1)} collective-permute-done((bf16[48,1024]{1,0:T(8,128)(2,1)S(1)}, bf16[48,1024]{1,0:T(8,128)(2,1)S(1)}, u32[]{:S(2)}, u32[]{:S(2)}) %collective-permute-start.21) | collective-permute-done | bytes 98336 | tf_op jit(solution)/shard_map/ppermute | solution.py:271
  224.1 2.8 adamw.13
  226.9 2.8 adamw.14
  229.6 4.1 collective-permute-done.23.refs_2_
  233.7 1.7 collective-permute-start.33
  235.5 3.8 adamw.15
  239.3 4.9 %adamw.16 = (bf16[256,3072]{1,0:T(8,128)(2,1)}, bf16[2,1024,3072]{2,1,0:T(8,128)(2,1)}, f32[2,256,3072]{2,1,0:T(8,128)}, f32[2,256,3072]{2,1,0:T(8,128)}) custom-call(s32[1]{0:T(128)} %bitcast.me, bf16[1,2,1024,3072]{3,2,1,0:T(8,128)(2,1)} %refs_0_.15, ...), custom_call_target="tpu_custom_call", output_to_operand_aliasing={{0}: (7, {}), {1}: (8, {}), {2}: (9, {}), {3}: (10, {})} | custom-call | flops 5505024 | bytes 11010048 | tf_op jit(solution)/shard_map/adamw/pallas_call | solution.py:177
  244.2 0.3 collective-permute-start.5
  244.5 0.5 collective-permute-start.29
  245.0 2.5 collective-permute-done.29.refs_0_
  247.8 1.7 collective-permute-start.36
  249.6 9.2 %adamw.18 = (bf16[256,3072]{1,0:T(8,128)(2,1)}, bf16[2,1024,3072]{2,1,0:T(8,128)(2,1)}, f32[2,256,3072]{2,1,0:T(8,128)}, f32[2,256,3072]{2,1,0:T(8,128)}) custom-call(s32[1]{0:T(128)} %bitcast.me, bf16[1,2,1024,3072]{3,2,1,0:T(8,128)(2,1)} %refs_1_.15, bf16[256,3072]{1,0:T(8,128)(2,1)} %get-tuple-element.101.near, bf16[256,3072]{1,0:T(8,128)(2,1)} %copy-done.2, ...), custom_call_target="tpu_custom_call" | custom-call | flops 11010048 | bytes 22020096 | tf_op jit(solution)/shard_map/adamw/pallas_call | solution.py:177
  258.8 9.4 %adamw.19 = (bf16[256,3072]{1,0:T(8,128)(2,1)}, bf16[2,1024,3072]{2,1,0:T(8,128)(2,1)}, f32[2,256,3072]{2,1,0:T(8,128)}, f32[2,256,3072]{2,1,0:T(8,128)}) custom-call(s32[1]{0:T(128)} %bitcast.me, bf16[1,2,1024,3072]{3,2,1,0:T(8,128)(2,1)} %refs_1_.15, ...), custom_call_target="tpu_custom_call", output_to_operand_aliasing={{1}: (7, {}), {2}: (8, {}), {3}: (9, {})} | custom-call | flops 11010048 | bytes 22020096 | tf_op jit(solution)/shard_map/adamw/pallas_call | solution.py:177
  268.6 19.6 %collective-permute-done.5.refs_1_ = bf16[256,3072]{1,0:T(8,128)(2,1)} collective-permute-done((bf16[256,3072]{1,0:T(8,128)(2,1)}, bf16[256,3072]{1,0:T(8,128)(2,1)}, u32[]{:S(2)}, u32[]{:S(2)}) %collective-permute-start.5) | collective-permute-done | bytes 1572896 | tf_op jit(solution)/shard_map/ppermute | solution.py:271
  288.2 33.7 %collective-permute-done.36.refs_1_ = bf16[768,1024]{1,0:T(8,128)(2,1)} collective-permute-done((bf16[768,1024]{1,0:T(8,128)(2,1)}, bf16[768,1024]{1,0:T(8,128)(2,1)}, u32[]{:S(2)}, u32[]{:S(2)}) %collective-permute-start.36) | collective-permute-done | bytes 1572896 | tf_op jit(solution)/shard_map/ppermute | solution.py:271
  321.9 1.7 collective-permute-start.13
  323.6 9.3 %adamw.17 = (bf16[256,3072]{1,0:T(8,128)(2,1)}, bf16[2,1024,3072]{2,1,0:T(8,128)(2,1)}, f32[2,256,3072]{2,1,0:T(8,128)}, f32[2,256,3072]{2,1,0:T(8,128)}) custom-call(s32[1]{0:T(128)} %bitcast.me, bf16[1,2,1024,3072]{3,2,1,0:T(8,128)(2,1)} %refs_0_.15, ...), custom_call_target="tpu_custom_call", output_to_operand_aliasing={{1}: (7, {}), {2}: (8, {}), {3}: (9, {})} | custom-call | flops 11010048 | bytes 22020096 | tf_op jit(solution)/shard_map/adamw/pallas_call | solution.py:177
  332.9 0.3 collective-permute-start.9
  333.3 22.3 %collective-permute-done.17.refs_4_ = bf16[256,3072]{1,0:T(8,128)(2,1)} collective-permute-done((bf16[256,3072]{1,0:T(8,128)(2,1)}, bf16[256,3072]{1,0:T(8,128)(2,1)}, u32[]{:S(2)}, u32[]{:S(2)}) %collective-permute-start.17) | collective-permute-done | bytes 1572896 | tf_op jit(solution)/shard_map/ppermute | solution.py:271
  355.6 0.5 collective-permute-start.18
  356.1 33.2 %collective-permute-done.13.refs_1_ = bf16[256,3072]{1,0:T(8,128)(2,1)} collective-permute-done((bf16[256,3072]{1,0:T(8,128)(2,1)}, bf16[256,3072]{1,0:T(8,128)(2,1)}, u32[]{:S(2)}, u32[]{:S(2)}) %collective-permute-start.13) | collective-permute-done | bytes 1572896 | tf_op jit(solution)/shard_map/ppermute | solution.py:271
  389.3 0.5 collective-permute-start.4
  389.8 31.4 %collective-permute-done.9.refs_4_ = bf16[256,3072]{1,0:T(8,128)(2,1)} collective-permute-done((bf16[256,3072]{1,0:T(8,128)(2,1)}, bf16[256,3072]{1,0:T(8,128)(2,1)}, u32[]{:S(2)}, u32[]{:S(2)}) %collective-permute-start.9) | collective-permute-done | bytes 1572896 | tf_op jit(solution)/shard_map/ppermute | solution.py:271
  421.2 0.5 collective-permute-start.6
  421.8 0.7 copy-done.6
  422.4 0.5 copy-done.4
  422.9 1.1 copy-done.5
  424.1 0.5 collective-permute-start.38
  424.6 3.6 carry.7.refs_3_
  428.2 2.6 carry.8.refs_3_
  430.8 2.1 carry.9.refs_5_
  432.9 0.9 place.2.refs_3_
  433.8 0.7 place.3
  434.6 7.3 %carry.6 = bf16[2,1024,3072]{2,1,0:T(8,128)(2,1)} custom-call(s32[1]{0:T(128)} %bitcast.me, bf16[256,3072]{1,0:T(8,128)(2,1)} %copy-done.3, bf16[256,3072]{1,0:T(8,128)(2,1)} %collective-permute-done.13.refs_1_, bf16[256,3072]{1,0:T(8,128)(2,1)} %copy-done.5, bf16[256,3072]{1,0:T(8,128)(2,1)} %collective-permute-done.16.refs_3_, ...), custom_call_target="tpu_custom_call", output_to_operand_aliasing={{}: (7, {})} | custom-call | flops 4718592 | bytes 18874368 | tf_op jit(solution)/shard_map/carry/pallas_call | solution.py:249
  441.8 0.7 bitcast_dynamic-update-slice_fusion
  442.5 7.3 %carry.5 = bf16[2,1024,3072]{2,1,0:T(8,128)(2,1)} custom-call(s32[1]{0:T(128)} %bitcast.me, bf16[256,3072]{1,0:T(8,128)(2,1)} %collective-permute-done.4.refs_0_, bf16[256,3072]{1,0:T(8,128)(2,1)} %collective-permute-done.5.refs_1_, bf16[256,3072]{1,0:T(8,128)(2,1)} %collective-permute-done.6.refs_2_, ...), custom_call_target="tpu_custom_call", output_to_operand_aliasing={{}: (7, {})} | custom-call | flops 4718592 | bytes 18874368 | tf_op jit(solution)/shard_map/carry/pallas_call | solution.py:249
  (72 shorter events, 1.3 us)
Async XLA Ops:
  7.3 87.5 %collective-permute-start.20 = (bf16[768,1024]{1,0:T(8,128)(2,1)}, bf16[768,1024]{1,0:T(8,128)(2,1)}, u32[]{:S(2)}, u32[]{:S(2)}) collective-permute-start(bf16[768,1024]{1,0:T(8,128)(2,1)} %get-tuple-element.114), channel_id=1, source_target_pairs={{0,2},{2,0},{1,3},{3,1},{4,6},{6,4},{5,7},{7,5}} | collective-permute-start | bytes 4718600 | tf_op jit(solution)/shard_map/ppermute | solution.py:271
  16.3 81.4 %collective-permute-start.19 = (bf16[768,1024]{1,0:T(8,128)(2,1)}, bf16[768,1024]{1,0:T(8,128)(2,1)S(1)}, u32[]{:S(2)}, u32[]{:S(2)}) collective-permute-start(bf16[768,1024]{1,0:T(8,128)(2,1)} %get-tuple-element.112), channel_id=1, source_target_pairs={{0,2},{2,0},{1,3},{3,1},{4,6},{6,4},{5,7},{7,5}} | collective-permute-start | bytes 4718600 | tf_op jit(solution)/shard_map/ppermute | solution.py:271
  18.1 65.5 %collective-permute-start.3 = (bf16[32,3072]{1,0:T(8,128)(2,1)S(1)}, bf16[32,3072]{1,0:T(8,128)(2,1)}, u32[]{:S(2)}, u32[]{:S(2)}) collective-permute-start(bf16[32,3072]{1,0:T(8,128)(2,1)S(1)} %first_pair.1), channel_id=1, source_target_pairs={{0,2},{2,0},{1,3},{3,1},{4,6},{6,4},{5,7},{7,5}} | collective-permute-start | bytes 589832 | tf_op jit(solution)/shard_map/ppermute | solution.py:271
  22.6 65.2 %collective-permute-start.2 = (bf16[32,3072]{1,0:T(8,128)(2,1)}, bf16[32,3072]{1,0:T(8,128)(2,1)S(1)}, u32[]{:S(2)}, u32[]{:S(2)}) collective-permute-start(bf16[32,3072]{1,0:T(8,128)(2,1)} %pair.10), channel_id=1, source_target_pairs={{0,2},{2,0},{1,3},{3,1},{4,6},{6,4},{5,7},{7,5}} | collective-permute-start | bytes 589832 | tf_op jit(solution)/shard_map/ppermute | solution.py:271
  28.8 185.4 %collective-permute-start.11 = (bf16[256,3072]{1,0:T(8,128)(2,1)}, bf16[256,3072]{1,0:T(8,128)(2,1)S(1)}, u32[]{:S(2)}, u32[]{:S(2)}) collective-permute-start(bf16[256,3072]{1,0:T(8,128)(2,1)} %get-tuple-element.102), channel_id=1, source_target_pairs={{0,2},{2,0},{1,3},{3,1},{4,6},{6,4},{5,7},{7,5}} | collective-permute-start | bytes 4718600 | tf_op jit(solution)/shard_map/ppermute | solution.py:271
  83.6 132.3 %collective-permute-start.15 = (bf16[256,3072]{1,0:T(8,128)(2,1)}, bf16[256,3072]{1,0:T(8,128)(2,1)}, u32[]{:S(2)}, u32[]{:S(2)}) collective-permute-start(bf16[256,3072]{1,0:T(8,128)(2,1)} %get-tuple-element.105), channel_id=1, source_target_pairs={{0,2},{2,0},{1,3},{3,1},{4,6},{6,4},{5,7},{7,5}} | collective-permute-start | bytes 4718600 | tf_op jit(solution)/shard_map/ppermute | solution.py:271
  87.7 7.0 %copy-start.11 = (bf16[32,3072]{1,0:T(8,128)(2,1)}, bf16[32,3072]{1,0:T(8,128)(2,1)S(1)}, u32[]{:S(2)}) copy-start(bf16[32,3072]{1,0:T(8,128)(2,1)S(1)} %collective-permute-done.2.far) | copy-start | bytes 589828
  87.7 128.2 %collective-permute-start.7 = (bf16[256,3072]{1,0:T(8,128)(2,1)}, bf16[256,3072]{1,0:T(8,128)(2,1)}, u32[]{:S(2)}, u32[]{:S(2)}) collective-permute-start(bf16[256,3072]{1,0:T(8,128)(2,1)} %get-tuple-element.95), channel_id=1, source_target_pairs={{0,2},{2,0},{1,3},{3,1},{4,6},{6,4},{5,7},{7,5}} | collective-permute-start | bytes 4718600 | tf_op jit(solution)/shard_map/ppermute | solution.py:271
  94.8 118.9 %collective-permute-start = (bf16[128,3072]{1,0:T(8,128)(2,1)}, bf16[128,3072]{1,0:T(8,128)(2,1)}, u32[]{:S(2)}, u32[]{:S(2)}) collective-permute-start(bf16[128,3072]{1,0:T(8,128)(2,1)} %get-tuple-element.77), channel_id=1, source_target_pairs={{0,2},{2,0},{1,3},{3,1},{4,6},{6,4},{5,7},{7,5}} | collective-permute-start | bytes 2359304 | tf_op jit(solution)/shard_map/ppermute | solution.py:271
  97.7 11.2 %copy-start = (bf16[768,1024]{1,0:T(8,128)(2,1)}, bf16[768,1024]{1,0:T(8,128)(2,1)S(1)}, u32[]{:S(2)}) copy-start(bf16[768,1024]{1,0:T(8,128)(2,1)S(1)} %collective-permute-done.19.far) | copy-start | bytes 4718596
  97.7 116.0 %collective-permute-start.1 = (bf16[64,3072]{1,0:T(8,128)(2,1)}, bf16[64,3072]{1,0:T(8,128)(2,1)}, u32[]{:S(2)}, u32[]{:S(2)}) collective-permute-start(bf16[64,3072]{1,0:T(8,128)(2,1)} %pair.9), channel_id=1, source_target_pairs={{0,2},{2,0},{1,3},{3,1},{4,6},{6,4},{5,7},{7,5}} | collective-permute-start | bytes 1179656 | tf_op jit(solution)/shard_map/ppermute | solution.py:271
  122.6 91.1 %copy-start.13 = (bf16[48,1024]{1,0:T(8,128)(2,1)S(1)}, bf16[48,1024]{1,0:T(8,128)(2,1)}, u32[]{:S(2)}) copy-start(bf16[48,1024]{1,0:T(8,128)(2,1)} %get-tuple-element.127) | copy-start | bytes 294916
  122.6 91.6 %copy-start.12 = (bf16[96,1024]{1,0:T(8,128)(2,1)S(1)}, bf16[96,1024]{1,0:T(8,128)(2,1)}, u32[]{:S(2)}) copy-start(bf16[96,1024]{1,0:T(8,128)(2,1)} %get-tuple-element.132) | copy-start | bytes 589828
  213.7 2.6 collective-permute-start.28
  213.7 4.3 collective-permute-start.27
  214.2 12.7 %copy-start.2 = (bf16[256,3072]{1,0:T(8,128)(2,1)}, bf16[256,3072]{1,0:T(8,128)(2,1)S(1)}, u32[]{:S(2)}) copy-start(bf16[256,3072]{1,0:T(8,128)(2,1)S(1)} %collective-permute-done.11.far) | copy-start | bytes 4718596
  214.2 29.9 %collective-permute-start.25 = (bf16[96,1024]{1,0:T(8,128)(2,1)S(1)}, bf16[96,1024]{1,0:T(8,128)(2,1)S(1)}, u32[]{:S(2)}, u32[]{:S(2)}) collective-permute-start(bf16[96,1024]{1,0:T(8,128)(2,1)S(1)} %copy-done.12), channel_id=1, source_target_pairs={{0,2},{2,0},{1,3},{3,1},{4,6},{6,4},{5,7},{7,5}} | collective-permute-start | bytes 589832 | tf_op jit(solution)/shard_map/ppermute | solution.py:271
  216.0 28.5 %collective-permute-start.24 = (bf16[96,1024]{1,0:T(8,128)(2,1)S(1)}, bf16[96,1024]{1,0:T(8,128)(2,1)S(1)}, u32[]{:S(2)}, u32[]{:S(2)}) collective-permute-start(bf16[96,1024]{1,0:T(8,128)(2,1)S(1)} %copy-done.12), channel_id=1, source_target_pairs={{0,1},{1,0},{2,3},{3,2},{4,5},{5,4},{6,7},{7,6}} | collective-permute-start | bytes 589832 | tf_op jit(solution)/shard_map/ppermute | solution.py:271
  216.0 8.1 %collective-permute-start.21 = (bf16[48,1024]{1,0:T(8,128)(2,1)S(1)}, bf16[48,1024]{1,0:T(8,128)(2,1)S(1)}, u32[]{:S(2)}, u32[]{:S(2)}) collective-permute-start(bf16[48,1024]{1,0:T(8,128)(2,1)S(1)} %copy-done.13), channel_id=1, source_target_pairs={{0,2},{2,0},{1,3},{3,1},{4,6},{6,4},{5,7},{7,5}} | collective-permute-start | bytes 294920 | tf_op jit(solution)/shard_map/ppermute | solution.py:271
  216.3 28.7 %collective-permute-start.30 = (bf16[192,1024]{1,0:T(8,128)(2,1)}, bf16[192,1024]{1,0:T(8,128)(2,1)}, u32[]{:S(2)}, u32[]{:S(2)}) collective-permute-start(bf16[192,1024]{1,0:T(8,128)(2,1)} %get-tuple-element.133), channel_id=1, source_target_pairs={{0,2},{2,0},{1,3},{3,1},{4,6},{6,4},{5,7},{7,5}} | collective-permute-start | bytes 1179656 | tf_op jit(solution)/shard_map/ppermute | solution.py:271
  218.1 15.7 %collective-permute-start.23 = (bf16[48,1024]{1,0:T(8,128)(2,1)}, bf16[48,1024]{1,0:T(8,128)(2,1)S(1)}, u32[]{:S(2)}, u32[]{:S(2)}) collective-permute-start(bf16[48,1024]{1,0:T(8,128)(2,1)} %get-tuple-element.131), channel_id=1, source_target_pairs={{0,2},{2,0},{1,3},{3,1},{4,6},{6,4},{5,7},{7,5}} | collective-permute-start | bytes 294920 | tf_op jit(solution)/shard_map/ppermute | solution.py:271
  224.1 20.4 %collective-permute-start.22 = (bf16[48,1024]{1,0:T(8,128)(2,1)S(1)}, bf16[48,1024]{1,0:T(8,128)(2,1)S(1)}, u32[]{:S(2)}, u32[]{:S(2)}) collective-permute-start(bf16[48,1024]{1,0:T(8,128)(2,1)S(1)} %collective-permute-done.21.refs_0_), channel_id=1, source_target_pairs={{0,1},{1,0},{2,3},{3,2},{4,5},{5,4},{6,7},{7,6}} | collective-permute-start | bytes 294920 | tf_op jit(solution)/shard_map/ppermute | solution.py:271
  233.7 25.0 %collective-permute-start.33 = (bf16[384,1024]{1,0:T(8,128)(2,1)}, bf16[384,1024]{1,0:T(8,128)(2,1)S(1)}, u32[]{:S(2)}, u32[]{:S(2)}) collective-permute-start(bf16[384,1024]{1,0:T(8,128)(2,1)} %get-tuple-element.134), channel_id=1, source_target_pairs={{0,2},{2,0},{1,3},{3,1},{4,6},{6,4},{5,7},{7,5}} | collective-permute-start | bytes 2359304 | tf_op jit(solution)/shard_map/ppermute | solution.py:271
  244.2 44.0 %collective-permute-start.5 = (bf16[256,3072]{1,0:T(8,128)(2,1)}, bf16[256,3072]{1,0:T(8,128)(2,1)}, u32[]{:S(2)}, u32[]{:S(2)}) collective-permute-start(bf16[256,3072]{1,0:T(8,128)(2,1)} %get-tuple-element.93), channel_id=1, source_target_pairs={{0,2},{2,0},{1,3},{3,1},{4,6},{6,4},{5,7},{7,5}} | collective-permute-start | bytes 4718600 | tf_op jit(solution)/shard_map/ppermute | solution.py:271
  244.5 23.7 %collective-permute-start.32 = (bf16[384,1024]{1,0:T(8,128)(2,1)}, bf16[384,1024]{1,0:T(8,128)(2,1)S(1)}, u32[]{:S(2)}, u32[]{:S(2)}) collective-permute-start(bf16[384,1024]{1,0:T(8,128)(2,1)} %get-tuple-element.134), channel_id=1, source_target_pairs={{0,1},{1,0},{2,3},{3,2},{4,5},{5,4},{6,7},{7,6}} | collective-permute-start | bytes 2359304 | tf_op jit(solution)/shard_map/ppermute | solution.py:271
  244.5 3.0 collective-permute-start.29
  245.0 2.8 collective-permute-start.26
  247.6 11.2 %copy-start.9 = (bf16[192,1024]{1,0:T(8,128)(2,1)}, bf16[192,1024]{1,0:T(8,128)(2,1)S(1)}, u32[]{:S(2)}) copy-start(bf16[192,1024]{1,0:T(8,128)(2,1)S(1)} %collective-permute-done.29.refs_0_) | copy-start | bytes 1179652
  247.6 21.0 %collective-permute-start.31 = (bf16[192,1024]{1,0:T(8,128)(2,1)}, bf16[192,1024]{1,0:T(8,128)(2,1)S(1)}, u32[]{:S(2)}, u32[]{:S(2)}) collective-permute-start(bf16[192,1024]{1,0:T(8,128)(2,1)} %collective-permute-done.30.refs_1_), channel_id=1, source_target_pairs={{0,1},{1,0},{2,3},{3,2},{4,5},{5,4},{6,7},{7,6}} | collective-permute-start | bytes 1179656 | tf_op jit(solution)/shard_map/ppermute | solution.py:271
  247.8 74.0 %collective-permute-start.36 = (bf16[768,1024]{1,0:T(8,128)(2,1)}, bf16[768,1024]{1,0:T(8,128)(2,1)}, u32[]{:S(2)}, u32[]{:S(2)}) collective-permute-start(bf16[768,1024]{1,0:T(8,128)(2,1)} %get-tuple-element.135), channel_id=1, source_target_pairs={{0,2},{2,0},{1,3},{3,1},{4,6},{6,4},{5,7},{7,5}} | collective-permute-start | bytes 4718600 | tf_op jit(solution)/shard_map/ppermute | solution.py:271
  258.8 29.4 %copy-start.7 = (bf16[384,1024]{1,0:T(8,128)(2,1)}, bf16[384,1024]{1,0:T(8,128)(2,1)S(1)}, u32[]{:S(2)}) copy-start(bf16[384,1024]{1,0:T(8,128)(2,1)S(1)} %collective-permute-done.33.refs_1_) | copy-start | bytes 2359300
  258.8 74.1 %collective-permute-start.35 = (bf16[768,1024]{1,0:T(8,128)(2,1)}, bf16[768,1024]{1,0:T(8,128)(2,1)}, u32[]{:S(2)}, u32[]{:S(2)}) collective-permute-start(bf16[768,1024]{1,0:T(8,128)(2,1)} %get-tuple-element.135), channel_id=1, source_target_pairs={{0,1},{1,0},{2,3},{3,2},{4,5},{5,4},{6,7},{7,6}} | collective-permute-start | bytes 4718600 | tf_op jit(solution)/shard_map/ppermute | solution.py:271
  268.2 55.4 %copy-start.8 = (bf16[384,1024]{1,0:T(8,128)(2,1)}, bf16[384,1024]{1,0:T(8,128)(2,1)S(1)}, u32[]{:S(2)}) copy-start(bf16[384,1024]{1,0:T(8,128)(2,1)S(1)} %collective-permute-done.32.refs_0_) | copy-start | bytes 2359300
  268.2 87.3 %collective-permute-start.17 = (bf16[256,3072]{1,0:T(8,128)(2,1)}, bf16[256,3072]{1,0:T(8,128)(2,1)}, u32[]{:S(2)}, u32[]{:S(2)}) collective-permute-start(bf16[256,3072]{1,0:T(8,128)(2,1)} %get-tuple-element.109), channel_id=1, source_target_pairs={{0,2},{2,0},{1,3},{3,1},{4,6},{6,4},{5,7},{7,5}} | collective-permute-start | bytes 4718600 | tf_op jit(solution)/shard_map/ppermute | solution.py:271
  268.5 55.1 %copy-start.10 = (bf16[192,1024]{1,0:T(8,128)(2,1)}, bf16[192,1024]{1,0:T(8,128)(2,1)S(1)}, u32[]{:S(2)}) copy-start(bf16[192,1024]{1,0:T(8,128)(2,1)S(1)} %collective-permute-done.31.refs_2_) | copy-start | bytes 1179652
  268.5 87.0 %collective-permute-start.16 = (bf16[256,3072]{1,0:T(8,128)(2,1)}, bf16[256,3072]{1,0:T(8,128)(2,1)}, u32[]{:S(2)}, u32[]{:S(2)}) collective-permute-start(bf16[256,3072]{1,0:T(8,128)(2,1)} %get-tuple-element.109), channel_id=1, source_target_pairs={{0,1},{1,0},{2,3},{3,2},{4,5},{5,4},{6,7},{7,6}} | collective-permute-start | bytes 4718600 | tf_op jit(solution)/shard_map/ppermute | solution.py:271
  288.2 44.8 %collective-permute-start.34 = (bf16[384,1024]{1,0:T(8,128)(2,1)S(1)}, bf16[384,1024]{1,0:T(8,128)(2,1)}, u32[]{:S(2)}, u32[]{:S(2)}) collective-permute-start(bf16[384,1024]{1,0:T(8,128)(2,1)S(1)} %collective-permute-done.33.refs_1_), channel_id=1, source_target_pairs={{0,1},{1,0},{2,3},{3,2},{4,5},{5,4},{6,7},{7,6}} | collective-permute-start | bytes 2359304 | tf_op jit(solution)/shard_map/ppermute | solution.py:271
  321.9 67.4 %collective-permute-start.13 = (bf16[256,3072]{1,0:T(8,128)(2,1)}, bf16[256,3072]{1,0:T(8,128)(2,1)}, u32[]{:S(2)}, u32[]{:S(2)}) collective-permute-start(bf16[256,3072]{1,0:T(8,128)(2,1)} %get-tuple-element.103), channel_id=1, source_target_pairs={{0,2},{2,0},{1,3},{3,1},{4,6},{6,4},{5,7},{7,5}} | collective-permute-start | bytes 4718600 | tf_op jit(solution)/shard_map/ppermute | solution.py:271
  323.6 65.7 %copy-start.1 = (bf16[256,3072]{1,0:T(8,128)(2,1)S(1)}, bf16[256,3072]{1,0:T(8,128)(2,1)}, u32[]{:S(2)}) copy-start(bf16[256,3072]{1,0:T(8,128)(2,1)} %get-tuple-element.93) | copy-start | bytes 4718596
  332.9 56.4 %collective-permute-start.12 = (bf16[256,3072]{1,0:T(8,128)(2,1)}, bf16[256,3072]{1,0:T(8,128)(2,1)S(1)}, u32[]{:S(2)}, u32[]{:S(2)}) collective-permute-start(bf16[256,3072]{1,0:T(8,128)(2,1)} %get-tuple-element.103), channel_id=1, source_target_pairs={{0,1},{1,0},{2,3},{3,2},{4,5},{5,4},{6,7},{7,6}} | collective-permute-start | bytes 4718600 | tf_op jit(solution)/shard_map/ppermute | solution.py:271
  332.9 88.2 %collective-permute-start.9 = (bf16[256,3072]{1,0:T(8,128)(2,1)}, bf16[256,3072]{1,0:T(8,128)(2,1)}, u32[]{:S(2)}, u32[]{:S(2)}) collective-permute-start(bf16[256,3072]{1,0:T(8,128)(2,1)} %get-tuple-element.99), channel_id=1, source_target_pairs={{0,2},{2,0},{1,3},{3,1},{4,6},{6,4},{5,7},{7,5}} | collective-permute-start | bytes 4718600 | tf_op jit(solution)/shard_map/ppermute | solution.py:271
  355.6 65.6 %collective-permute-start.37 = (bf16[768,1024]{1,0:T(8,128)(2,1)}, bf16[768,1024]{1,0:T(8,128)(2,1)S(1)}, u32[]{:S(2)}, u32[]{:S(2)}) collective-permute-start(bf16[768,1024]{1,0:T(8,128)(2,1)} %collective-permute-done.36.refs_1_), channel_id=1, source_target_pairs={{0,1},{1,0},{2,3},{3,2},{4,5},{5,4},{6,7},{7,6}} | collective-permute-start | bytes 4718600 | tf_op jit(solution)/shard_map/ppermute | solution.py:271
  355.6 66.1 %collective-permute-start.18 = (bf16[256,3072]{1,0:T(8,128)(2,1)}, bf16[256,3072]{1,0:T(8,128)(2,1)S(1)}, u32[]{:S(2)}, u32[]{:S(2)}) collective-permute-start(bf16[256,3072]{1,0:T(8,128)(2,1)} %collective-permute-done.17.refs_4_), channel_id=1, source_target_pairs={{0,1},{1,0},{2,3},{3,2},{4,5},{5,4},{6,7},{7,6}} | collective-permute-start | bytes 4718600 | tf_op jit(solution)/shard_map/ppermute | solution.py:271
  389.3 32.5 %collective-permute-start.14 = (bf16[256,3072]{1,0:T(8,128)(2,1)}, bf16[256,3072]{1,0:T(8,128)(2,1)S(1)}, u32[]{:S(2)}, u32[]{:S(2)}) collective-permute-start(bf16[256,3072]{1,0:T(8,128)(2,1)} %collective-permute-done.13.refs_1_), channel_id=1, source_target_pairs={{0,1},{1,0},{2,3},{3,2},{4,5},{5,4},{6,7},{7,6}} | collective-permute-start | bytes 4718600 | tf_op jit(solution)/shard_map/ppermute | solution.py:271
  389.3 32.5 %copy-start.3 = (bf16[256,3072]{1,0:T(8,128)(2,1)}, bf16[256,3072]{1,0:T(8,128)(2,1)S(1)}, u32[]{:S(2)}) copy-start(bf16[256,3072]{1,0:T(8,128)(2,1)S(1)} %collective-permute-done.12.refs_0_) | copy-start | bytes 4718596
  389.3 53.2 %collective-permute-start.4 = (bf16[256,3072]{1,0:T(8,128)(2,1)S(1)}, bf16[256,3072]{1,0:T(8,128)(2,1)}, u32[]{:S(2)}, u32[]{:S(2)}) collective-permute-start(bf16[256,3072]{1,0:T(8,128)(2,1)S(1)} %copy-done.1), channel_id=1, source_target_pairs={{0,1},{1,0},{2,3},{3,2},{4,5},{5,4},{6,7},{7,6}} | collective-permute-start | bytes 4718600 | tf_op jit(solution)/shard_map/ppermute | solution.py:271
  421.2 21.3 %collective-permute-start.8 = (bf16[256,3072]{1,0:T(8,128)(2,1)}, bf16[256,3072]{1,0:T(8,128)(2,1)}, u32[]{:S(2)}, u32[]{:S(2)}) collective-permute-start(bf16[256,3072]{1,0:T(8,128)(2,1)} %get-tuple-element.99), channel_id=1, source_target_pairs={{0,1},{1,0},{2,3},{3,2},{4,5},{5,4},{6,7},{7,6}} | collective-permute-start | bytes 4718600 | tf_op jit(solution)/shard_map/ppermute | solution.py:271
  421.2 1.2 copy-start.6
  421.2 21.3 %collective-permute-start.6 = (bf16[256,3072]{1,0:T(8,128)(2,1)}, bf16[256,3072]{1,0:T(8,128)(2,1)}, u32[]{:S(2)}, u32[]{:S(2)}) collective-permute-start(bf16[256,3072]{1,0:T(8,128)(2,1)} %collective-permute-done.5.refs_1_), channel_id=1, source_target_pairs={{0,1},{1,0},{2,3},{3,2},{4,5},{5,4},{6,7},{7,6}} | collective-permute-start | bytes 4718600 | tf_op jit(solution)/shard_map/ppermute | solution.py:271
  421.7 1.2 copy-start.4
  421.7 20.8 %collective-permute-start.10 = (bf16[256,3072]{1,0:T(8,128)(2,1)}, bf16[256,3072]{1,0:T(8,128)(2,1)}, u32[]{:S(2)}, u32[]{:S(2)}) collective-permute-start(bf16[256,3072]{1,0:T(8,128)(2,1)} %collective-permute-done.9.refs_4_), channel_id=1, source_target_pairs={{0,1},{1,0},{2,3},{3,2},{4,5},{5,4},{6,7},{7,6}} | collective-permute-start | bytes 4718600 | tf_op jit(solution)/shard_map/ppermute | solution.py:271
  422.9 1.1 copy-start.5
  424.1 17.8 %collective-permute-start.38 = (bf16[48,1024]{1,0:T(8,128)(2,1)S(1)}, bf16[48,1024]{1,0:T(8,128)(2,1)S(1)}, u32[]{:S(2)}, u32[]{:S(2)}) collective-permute-start(bf16[48,1024]{1,0:T(8,128)(2,1)S(1)} %collective-permute-done.23.refs_2_), channel_id=1, source_target_pairs={{0,1},{1,0},{2,3},{3,2},{4,5},{5,4},{6,7},{7,6}} | collective-permute-start | bytes 294920 | tf_op jit(solution)/shard_map/ppermute | solution.py:271

commit v2 on v0

--- a/solution.py
+++ b/solution.py
@@ -62,15 +62,16 @@
         for i, c in enumerate(nears)
     ]
     outs = [pltpu.make_async_copy(total.at[pl.ds(t * tile, tile)], both.at[pl.ds(t * tile, tile)], out_sem.at[t]) for t in range(count)]
+    for own in owns:
+        own.start()
     pl.semaphore_wait(barrier, 1)
-    for far, own in zip(fars, owns):
+    for far in fars:
         far.start()
-        own.start()
     for copy in beside:
         copy.start()
     for t in range(count):
+        fars[t].wait_recv()
         owns[t].wait()
-        fars[t].wait_recv()
         here = pl.ds(t * tile, tile)
         total[here] = (got[here].astype(jnp.float32) + mine[here].astype(jnp.float32)).astype(jnp.bfloat16)
         outs[t].start()
@@ -97,8 +98,8 @@
     own.start()
     pl.semaphore_wait(barrier, 1)
     far.start()
+    far.wait_recv()
     own.wait()
-    far.wait_recv()
     both[...] = (got[...].astype(jnp.float32) + mine[...].astype(jnp.float32)).astype(jnp.bfloat16)
     far.wait_send()
 
@@ -119,7 +120,7 @@
 
 
 def pair_tile(rows, cols):
-    return rows if rows * cols <= 96 * 3072 else math.gcd(rows, 64 * 3072 // cols)
+    return rows if rows * cols <= 96 * 3072 else math.gcd(rows, 128 * 3072 // cols)
 
 
 def pair(terms, index, nears):
@@ -162,7 +163,7 @@
     _, layer, sum_first, _ = SUMS[r]
     _, _, chunk_first, chunk_rows = CHUNKS[c]
     block, cols = m.shape[1], m.shape[2]
-    tile = math.gcd(rows, first, block, first - sum_first, first - chunk_first, 128 * 3072 // cols)
+    tile = math.gcd(rows, first, block, first - sum_first, first - chunk_first, 64 * 3072 // cols)
     at, per = first // tile, block // tile
     of_sum, of_chunk = (first - sum_first) // tile, (first - chunk_first) // tile
     mine = pl.BlockSpec((1, tile, cols), lambda i, me: (layer, at + i, 0))

time: 462 us -> 461 us (level)
  no operation moved by 1% of the time
where the time goes in v2:
time: 461 us; the launch traced here: 460 us
  waiting for transfers between devices  295 us (64%)
  Pallas kernels  135 us (29%)
  starting transfers between devices  25.2 us (5%)
  local copies, waits for them, and re-layouts  4.61 us (1%)
    ppermute x39, waiting for transfers between devices, send(): return lax.ppermute(x, 'dp', to)  295 us
    pallas_call x13, Pallas kernels, adamw(): pl.pallas_call(functools.partial(adamw_body, len(have)), grid_spec=pltpu....  67.3 us
    pallas_call x8, Pallas kernels, pair(): pl.pallas_call(functools.partial(pair_body, chunk, nears), in_specs=[anyw...  41.2 us
    ppermute x39, starting transfers between devices, send(): return lax.ppermute(x, 'dp', to)  25.2 us
    pallas_call x7, Pallas kernels, carry(): pl.pallas_call(functools.partial(carry_body, chunk, block), in_specs=[pl....  22.8 us
  transfers between devices with their start and end apart: 39, of which 10 were waited for; matrix products, arithmetic and copies ran while one was open for 0% of the time, Pallas kernels for 27%

profile of v2, /device:TPU:0, one launch (start us, length us, event | category | flops | bytes accessed | tf_op | source)
XLA Modules:
  0.0 460.3 jit_solution(17952368761743641181)
XLA Ops:
  0.6 6.6 %pair.15 = (bf16[768,1024]{1,0:T(8,128)(2,1)}, bf16[768,1024]{1,0:T(8,128)(2,1)}) custom-call(bf16[1,2,1024,3072]{3,2,1,0:T(8,128)(2,1)} %refs_0_.15, bf16[1,2,1024,3072]{3,2,1,0:T(8,128)(2,1)} %refs_1_.15, bf16[1,2,3072,1024]{3,2,1,0:T(8,128)(2,1)} %own.25), custom_call_target="tpu_custom_call" | custom-call | flops 786432 | bytes 7864320 | tf_op jit(solution)/shard_map/pair/pallas_call | solution.py:133
  7.2 2.9 collective-permute-start.20
  10.1 6.1 %pair.14 = (bf16[768,1024]{1,0:T(8,128)(2,1)}, bf16[768,1024]{1,0:T(8,128)(2,1)}) custom-call(bf16[1,2,1024,3072]{3,2,1,0:T(8,128)(2,1)} %refs_0_.15, bf16[1,2,1024,3072]{3,2,1,0:T(8,128)(2,1)} %refs_1_.15, bf16[1,2,3072,1024]{3,2,1,0:T(8,128)(2,1)} %own.25), custom_call_target="tpu_custom_call" | custom-call | flops 786432 | bytes 7864320 | tf_op jit(solution)/shard_map/pair/pallas_call | solution.py:133
  16.2 1.7 first_pair.1
  18.0 2.0 collective-permute-start.4
  20.0 2.4 pair.11
  22.5 6.1 %pair.13 = (bf16[256,3072]{1,0:T(8,128)(2,1)}, bf16[256,3072]{1,0:T(8,128)(2,1)}) custom-call(bf16[1,2,1024,3072]{3,2,1,0:T(8,128)(2,1)} %refs_0_.15, bf16[1,2,1024,3072]{3,2,1,0:T(8,128)(2,1)} %refs_1_.15, bf16[1,2,3072,1024]{3,2,1,0:T(8,128)(2,1)} %own.25), custom_call_target="tpu_custom_call" | custom-call | flops 786432 | bytes 7864320 | tf_op jit(solution)/shard_map/pair/pallas_call | solution.py:133
  28.6 2.0 collective-permute-start.12
  30.6 6.1 %pair.12 = (bf16[256,3072]{1,0:T(8,128)(2,1)}, bf16[256,3072]{1,0:T(8,128)(2,1)}) custom-call(bf16[1,2,1024,3072]{3,2,1,0:T(8,128)(2,1)} %refs_0_.15, bf16[1,2,1024,3072]{3,2,1,0:T(8,128)(2,1)} %refs_1_.15, bf16[1,2,3072,1024]{3,2,1,0:T(8,128)(2,1)} %own.25), custom_call_target="tpu_custom_call" | custom-call | flops 786432 | bytes 7864320 | tf_op jit(solution)/shard_map/pair/pallas_call | solution.py:133
  36.7 46.9 %collective-permute-done.4.far = bf16[32,3072]{1,0:T(8,128)(2,1)} collective-permute-done((bf16[32,3072]{1,0:T(8,128)(2,1)S(1)}, bf16[32,3072]{1,0:T(8,128)(2,1)}, u32[]{:S(2)}, u32[]{:S(2)}) %collective-permute-start.4) | collective-permute-done | bytes 196640 | tf_op jit(solution)/shard_map/ppermute | solution.py:269
  83.6 2.0 collective-permute-start.11
  85.6 6.1 %pair.8 = (bf16[256,3072]{1,0:T(8,128)(2,1)}, bf16[256,3072]{1,0:T(8,128)(2,1)}) custom-call(bf16[1,2,1024,3072]{3,2,1,0:T(8,128)(2,1)} %refs_0_.15, bf16[1,2,1024,3072]{3,2,1,0:T(8,128)(2,1)} %refs_1_.15, bf16[1,2,3072,1024]{3,2,1,0:T(8,128)(2,1)} %own.25), custom_call_target="tpu_custom_call" | custom-call | flops 786432 | bytes 7864320 | tf_op jit(solution)/shard_map/pair/pallas_call | solution.py:133
  91.7 5.0 %pair.9 = (bf16[128,3072]{1,0:T(8,128)(2,1)}, bf16[32,3072]{1,0:T(8,128)(2,1)}, bf16[32,3072]{1,0:T(8,128)(2,1)}, bf16[64,3072]{1,0:T(8,128)(2,1)}, bf16[128,3072]{1,0:T(8,128)(2,1)}) custom-call(bf16[1,2,1024,3072]{3,2,1,0:T(8,128)(2,1)} %refs_0_.15, bf16[1,2,1024,3072]{3,2,1,0:T(8,128)(2,1)} %refs_1_.15, bf16[1,2,3072,1024]{3,2,1,0:T(8,128)(2,1)} %own.25), custom_call_target="tpu_custom_call" | custom-call | flops 393216 | bytes 3932160 | tf_op jit(solution)/shard_map/pair/pallas_call | solution.py:133
  96.8 2.0 collective-permute-start.1
  98.8 2.8 pair.10
  101.7 9.7 %adamw.20 = (bf16[768,1024]{1,0:T(8,128)(2,1)}, bf16[2,3072,1024]{2,1,0:T(8,128)(2,1)}, f32[2,768,1024]{2,1,0:T(8,128)}, f32[2,768,1024]{2,1,0:T(8,128)}) custom-call(s32[1]{0:T(128)} %bitcast.me, bf16[1,2,3072,1024]{3,2,1,0:T(8,128)(2,1)} %own.25, bf16[768,1024]{1,0:T(8,128)(2,1)} %get-tuple-element.113.near, ...), custom_call_target="tpu_custom_call" | custom-call | flops 11010048 | bytes 22020096 | tf_op jit(solution)/shard_map/adamw/pallas_call | solution.py:177
  111.4 4.9 %adamw.21 = (bf16[384,1024]{1,0:T(8,128)(2,1)}, bf16[2,3072,1024]{2,1,0:T(8,128)(2,1)}, f32[2,768,1024]{2,1,0:T(8,128)}, f32[2,768,1024]{2,1,0:T(8,128)}) custom-call(s32[1]{0:T(128)} %bitcast.me, bf16[1,2,3072,1024]{3,2,1,0:T(8,128)(2,1)} %own.25, ...), custom_call_target="tpu_custom_call", output_to_operand_aliasing={{1}: (7, {}), {2}: (8, {}), {3}: (9, {})} | custom-call | flops 5505024 | bytes 11010048 | tf_op jit(solution)/shard_map/adamw/pallas_call | solution.py:177
  116.3 3.8 adamw.22
  120.1 2.8 adamw.23
  122.8 2.2 adamw.24
  125.0 2.2 adamw.25
  127.2 86.4 %collective-permute-done.2.far = bf16[64,3072]{1,0:T(8,128)(2,1)} collective-permute-done((bf16[64,3072]{1,0:T(8,128)(2,1)}, bf16[64,3072]{1,0:T(8,128)(2,1)}, u32[]{:S(2)}, u32[]{:S(2)}) %collective-permute-start.2) | collective-permute-done | bytes 393248 | tf_op jit(solution)/shard_map/ppermute | solution.py:269
  213.6 0.5 collective-permute-start.27
  214.2 1.7 collective-permute-start.23
  216.2 1.7 collective-permute-start.33
  218.3 1.7 collective-permute-done.23.refs_2_
  220.0 22.3 %collective-permute-done.21.refs_0_ = bf16[48,1024]{1,0:T(8,128)(2,1)S(1)} collective-permute-done((bf16[48,1024]{1,0:T(8,128)(2,1)S(1)}, bf16[48,1024]{1,0:T(8,128)(2,1)S(1)}, u32[]{:S(2)}, u32[]{:S(2)}) %collective-permute-start.21) | collective-permute-done | bytes 98336 | tf_op jit(solution)/shard_map/ppermute | solution.py:269
  242.3 1.7 collective-permute-start.30
  244.0 2.8 adamw.13
  246.8 2.8 adamw.14
  249.5 3.8 adamw.15
  253.3 4.9 %adamw.16 = (bf16[256,3072]{1,0:T(8,128)(2,1)}, bf16[2,1024,3072]{2,1,0:T(8,128)(2,1)}, f32[2,256,3072]{2,1,0:T(8,128)}, f32[2,256,3072]{2,1,0:T(8,128)}) custom-call(s32[1]{0:T(128)} %bitcast.me, bf16[1,2,1024,3072]{3,2,1,0:T(8,128)(2,1)} %refs_0_.15, ...), custom_call_target="tpu_custom_call", output_to_operand_aliasing={{0}: (7, {}), {1}: (8, {}), {2}: (9, {}), {3}: (10, {})} | custom-call | flops 5505024 | bytes 11010048 | tf_op jit(solution)/shard_map/adamw/pallas_call | solution.py:177
  258.2 0.5 collective-permute-start.29
  259.1 1.3 collective-permute-done.29.beside
  260.7 0.4 copy-done.8
  261.5 0.9 collective-permute-start.36
  262.5 9.2 %adamw.18 = (bf16[256,3072]{1,0:T(8,128)(2,1)}, bf16[2,1024,3072]{2,1,0:T(8,128)(2,1)}, f32[2,256,3072]{2,1,0:T(8,128)}, f32[2,256,3072]{2,1,0:T(8,128)}) custom-call(s32[1]{0:T(128)} %bitcast.me, bf16[1,2,1024,3072]{3,2,1,0:T(8,128)(2,1)} %refs_1_.15, bf16[256,3072]{1,0:T(8,128)(2,1)} %get-tuple-element.103.near, bf16[256,3072]{1,0:T(8,128)(2,1)} %copy-done.1, ...), custom_call_target="tpu_custom_call" | custom-call | flops 11010048 | bytes 22020096 | tf_op jit(solution)/shard_map/adamw/pallas_call | solution.py:177
  271.7 1.1 collective-permute-start.17
  272.7 23.5 %collective-permute-done.9.across = bf16[256,3072]{1,0:T(8,128)(2,1)S(1)} collective-permute-done((bf16[256,3072]{1,0:T(8,128)(2,1)}, bf16[256,3072]{1,0:T(8,128)(2,1)S(1)}, u32[]{:S(2)}, u32[]{:S(2)}) %collective-permute-start.9) | collective-permute-done | bytes 1572896 | tf_op jit(solution)/shard_map/ppermute | solution.py:269
  296.3 0.5 collective-permute-start.16
  296.8 9.2 %adamw.19 = (bf16[256,3072]{1,0:T(8,128)(2,1)}, bf16[2,1024,3072]{2,1,0:T(8,128)(2,1)}, f32[2,256,3072]{2,1,0:T(8,128)}, f32[2,256,3072]{2,1,0:T(8,128)}) custom-call(s32[1]{0:T(128)} %bitcast.me, bf16[1,2,1024,3072]{3,2,1,0:T(8,128)(2,1)} %refs_1_.15, ...), custom_call_target="tpu_custom_call", output_to_operand_aliasing={{1}: (7, {}), {2}: (8, {}), {3}: (9, {})} | custom-call | flops 11010048 | bytes 22020096 | tf_op jit(solution)/shard_map/adamw/pallas_call | solution.py:177
  306.0 9.2 %adamw.17 = (bf16[256,3072]{1,0:T(8,128)(2,1)}, bf16[2,1024,3072]{2,1,0:T(8,128)(2,1)}, f32[2,256,3072]{2,1,0:T(8,128)}, f32[2,256,3072]{2,1,0:T(8,128)}) custom-call(s32[1]{0:T(128)} %bitcast.me, bf16[1,2,1024,3072]{3,2,1,0:T(8,128)(2,1)} %refs_0_.15, ...), custom_call_target="tpu_custom_call", output_to_operand_aliasing={{1}: (7, {}), {2}: (8, {}), {3}: (9, {})} | custom-call | flops 11010048 | bytes 22020096 | tf_op jit(solution)/shard_map/adamw/pallas_call | solution.py:177
  315.1 14.9 %collective-permute-done.36.across = bf16[768,1024]{1,0:T(8,128)(2,1)} collective-permute-done((bf16[768,1024]{1,0:T(8,128)(2,1)}, bf16[768,1024]{1,0:T(8,128)(2,1)}, u32[]{:S(2)}, u32[]{:S(2)}) %collective-permute-start.36) | collective-permute-done | bytes 1572896 | tf_op jit(solution)/shard_map/ppermute | solution.py:269
  330.4 1.7 collective-permute-start.6
  332.1 31.6 %collective-permute-done.17.across = bf16[256,3072]{1,0:T(8,128)(2,1)} collective-permute-done((bf16[256,3072]{1,0:T(8,128)(2,1)}, bf16[256,3072]{1,0:T(8,128)(2,1)}, u32[]{:S(2)}, u32[]{:S(2)}) %collective-permute-start.17) | collective-permute-done | bytes 1572896 | tf_op jit(solution)/shard_map/ppermute | solution.py:269
  363.8 0.5 collective-permute-start.18
  364.3 33.2 %collective-permute-done.14.across = bf16[256,3072]{1,0:T(8,128)(2,1)} collective-permute-done((bf16[256,3072]{1,0:T(8,128)(2,1)}, bf16[256,3072]{1,0:T(8,128)(2,1)}, u32[]{:S(2)}, u32[]{:S(2)}) %collective-permute-start.14) | collective-permute-done | bytes 1572896 | tf_op jit(solution)/shard_map/ppermute | solution.py:269
  397.5 32.8 %collective-permute-done.6.across = bf16[256,3072]{1,0:T(8,128)(2,1)} collective-permute-done((bf16[256,3072]{1,0:T(8,128)(2,1)}, bf16[256,3072]{1,0:T(8,128)(2,1)}, u32[]{:S(2)}, u32[]{:S(2)}) %collective-permute-start.6) | collective-permute-done | bytes 1572896 | tf_op jit(solution)/shard_map/ppermute | solution.py:269
  430.3 0.5 collective-permute-start.5
  430.8 0.6 copy-done.4
  431.4 0.6 copy-done.6
  432.0 1.1 copy-done.5
  433.2 0.5 collective-permute-start.38
  433.6 3.6 carry.11.before
  437.3 2.6 carry.12.before
  439.9 2.1 carry.13.refs_5_
  442.0 0.9 place.2.refs_3_
  442.9 3.6 carry.7.before
  446.5 0.7 place.3
  447.3 3.6 carry.9.before
  451.0 3.6 carry.10
  454.6 0.7 bitcast_dynamic-update-slice_fusion
  455.3 1.2 copy-done.3
  456.5 3.6 carry.8
  (72 shorter events, 2.4 us)
Async XLA Ops:
  7.2 89.5 %collective-permute-start.20 = (bf16[768,1024]{1,0:T(8,128)(2,1)}, bf16[768,1024]{1,0:T(8,128)(2,1)}, u32[]{:S(2)}, u32[]{:S(2)}) collective-permute-start(bf16[768,1024]{1,0:T(8,128)(2,1)} %get-tuple-element.114), channel_id=1, source_target_pairs={{0,2},{2,0},{1,3},{3,1},{4,6},{6,4},{5,7},{7,5}} | collective-permute-start | bytes 4718600 | tf_op jit(solution)/shard_map/ppermute | solution.py:269
  16.2 85.4 %collective-permute-start.19 = (bf16[768,1024]{1,0:T(8,128)(2,1)}, bf16[768,1024]{1,0:T(8,128)(2,1)S(1)}, u32[]{:S(2)}, u32[]{:S(2)}) collective-permute-start(bf16[768,1024]{1,0:T(8,128)(2,1)} %get-tuple-element.112), channel_id=1, source_target_pairs={{0,2},{2,0},{1,3},{3,1},{4,6},{6,4},{5,7},{7,5}} | collective-permute-start | bytes 4718600 | tf_op jit(solution)/shard_map/ppermute | solution.py:269
  18.0 65.6 %collective-permute-start.4 = (bf16[32,3072]{1,0:T(8,128)(2,1)S(1)}, bf16[32,3072]{1,0:T(8,128)(2,1)}, u32[]{:S(2)}, u32[]{:S(2)}) collective-permute-start(bf16[32,3072]{1,0:T(8,128)(2,1)S(1)} %first_pair.1), channel_id=1, source_target_pairs={{0,2},{2,0},{1,3},{3,1},{4,6},{6,4},{5,7},{7,5}} | collective-permute-start | bytes 589832 | tf_op jit(solution)/shard_map/ppermute | solution.py:269
  22.4 69.3 %collective-permute-start.3 = (bf16[32,3072]{1,0:T(8,128)(2,1)}, bf16[32,3072]{1,0:T(8,128)(2,1)S(1)}, u32[]{:S(2)}, u32[]{:S(2)}) collective-permute-start(bf16[32,3072]{1,0:T(8,128)(2,1)} %pair.11), channel_id=1, source_target_pairs={{0,2},{2,0},{1,3},{3,1},{4,6},{6,4},{5,7},{7,5}} | collective-permute-start | bytes 589832 | tf_op jit(solution)/shard_map/ppermute | solution.py:269
  28.6 185.6 %collective-permute-start.12 = (bf16[256,3072]{1,0:T(8,128)(2,1)}, bf16[256,3072]{1,0:T(8,128)(2,1)S(1)}, u32[]{:S(2)}, u32[]{:S(2)}) collective-permute-start(bf16[256,3072]{1,0:T(8,128)(2,1)} %get-tuple-element.104), channel_id=1, source_target_pairs={{0,2},{2,0},{1,3},{3,1},{4,6},{6,4},{5,7},{7,5}} | collective-permute-start | bytes 4718600 | tf_op jit(solution)/shard_map/ppermute | solution.py:269
  83.6 132.3 %collective-permute-start.11 = (bf16[256,3072]{1,0:T(8,128)(2,1)}, bf16[256,3072]{1,0:T(8,128)(2,1)}, u32[]{:S(2)}, u32[]{:S(2)}) collective-permute-start(bf16[256,3072]{1,0:T(8,128)(2,1)} %get-tuple-element.102), channel_id=1, source_target_pairs={{0,2},{2,0},{1,3},{3,1},{4,6},{6,4},{5,7},{7,5}} | collective-permute-start | bytes 4718600 | tf_op jit(solution)/shard_map/ppermute | solution.py:269
  91.7 5.1 %copy-start.10 = (bf16[32,3072]{1,0:T(8,128)(2,1)}, bf16[32,3072]{1,0:T(8,128)(2,1)S(1)}, u32[]{:S(2)}) copy-start(bf16[32,3072]{1,0:T(8,128)(2,1)S(1)} %collective-permute-done.3.far) | copy-start | bytes 589828
  91.7 124.5 %collective-permute-start = (bf16[256,3072]{1,0:T(8,128)(2,1)}, bf16[256,3072]{1,0:T(8,128)(2,1)}, u32[]{:S(2)}, u32[]{:S(2)}) collective-permute-start(bf16[256,3072]{1,0:T(8,128)(2,1)} %get-tuple-element.77), channel_id=1, source_target_pairs={{0,2},{2,0},{1,3},{3,1},{4,6},{6,4},{5,7},{7,5}} | collective-permute-start | bytes 4718600 | tf_op jit(solution)/shard_map/ppermute | solution.py:269
  96.8 116.9 %collective-permute-start.1 = (bf16[128,3072]{1,0:T(8,128)(2,1)}, bf16[128,3072]{1,0:T(8,128)(2,1)}, u32[]{:S(2)}, u32[]{:S(2)}) collective-permute-start(bf16[128,3072]{1,0:T(8,128)(2,1)} %get-tuple-element.79), channel_id=1, source_target_pairs={{0,2},{2,0},{1,3},{3,1},{4,6},{6,4},{5,7},{7,5}} | collective-permute-start | bytes 2359304 | tf_op jit(solution)/shard_map/ppermute | solution.py:269
  101.6 9.7 %copy-start = (bf16[768,1024]{1,0:T(8,128)(2,1)}, bf16[768,1024]{1,0:T(8,128)(2,1)S(1)}, u32[]{:S(2)}) copy-start(bf16[768,1024]{1,0:T(8,128)(2,1)S(1)} %collective-permute-done.19.far) | copy-start | bytes 4718596
  101.6 112.0 %collective-permute-start.2 = (bf16[64,3072]{1,0:T(8,128)(2,1)}, bf16[64,3072]{1,0:T(8,128)(2,1)}, u32[]{:S(2)}, u32[]{:S(2)}) collective-permute-start(bf16[64,3072]{1,0:T(8,128)(2,1)} %pair.10), channel_id=1, source_target_pairs={{0,2},{2,0},{1,3},{3,1},{4,6},{6,4},{5,7},{7,5}} | collective-permute-start | bytes 1179656 | tf_op jit(solution)/shard_map/ppermute | solution.py:269
  125.0 88.6 %copy-start.12 = (bf16[48,1024]{1,0:T(8,128)(2,1)S(1)}, bf16[48,1024]{1,0:T(8,128)(2,1)}, u32[]{:S(2)}) copy-start(bf16[48,1024]{1,0:T(8,128)(2,1)} %get-tuple-element.127) | copy-start | bytes 294916
  125.0 90.9 %copy-start.11 = (bf16[96,1024]{1,0:T(8,128)(2,1)S(1)}, bf16[96,1024]{1,0:T(8,128)(2,1)}, u32[]{:S(2)}) copy-start(bf16[96,1024]{1,0:T(8,128)(2,1)} %get-tuple-element.132) | copy-start | bytes 589828
  213.6 4.3 collective-permute-start.28
  213.6 4.3 collective-permute-start.27
  214.2 32.6 %copy-start.1 = (bf16[256,3072]{1,0:T(8,128)(2,1)}, bf16[256,3072]{1,0:T(8,128)(2,1)S(1)}, u32[]{:S(2)}) copy-start(bf16[256,3072]{1,0:T(8,128)(2,1)S(1)} %collective-permute-done.12.far) | copy-start | bytes 4718596
  214.2 5.8 %collective-permute-start.23 = (bf16[48,1024]{1,0:T(8,128)(2,1)}, bf16[48,1024]{1,0:T(8,128)(2,1)S(1)}, u32[]{:S(2)}, u32[]{:S(2)}) collective-permute-start(bf16[48,1024]{1,0:T(8,128)(2,1)} %get-tuple-element.131), channel_id=1, source_target_pairs={{0,2},{2,0},{1,3},{3,1},{4,6},{6,4},{5,7},{7,5}} | collective-permute-start | bytes 294920 | tf_op jit(solution)/shard_map/ppermute | solution.py:269
  215.9 28.1 %collective-permute-start.25 = (bf16[96,1024]{1,0:T(8,128)(2,1)S(1)}, bf16[96,1024]{1,0:T(8,128)(2,1)S(1)}, u32[]{:S(2)}, u32[]{:S(2)}) collective-permute-start(bf16[96,1024]{1,0:T(8,128)(2,1)S(1)} %copy-done.11), channel_id=1, source_target_pairs={{0,2},{2,0},{1,3},{3,1},{4,6},{6,4},{5,7},{7,5}} | collective-permute-start | bytes 589832 | tf_op jit(solution)/shard_map/ppermute | solution.py:269
  216.2 45.3 %collective-permute-start.33 = (bf16[384,1024]{1,0:T(8,128)(2,1)}, bf16[384,1024]{1,0:T(8,128)(2,1)}, u32[]{:S(2)}, u32[]{:S(2)}) collective-permute-start(bf16[384,1024]{1,0:T(8,128)(2,1)} %get-tuple-element.134), channel_id=1, source_target_pairs={{0,2},{2,0},{1,3},{3,1},{4,6},{6,4},{5,7},{7,5}} | collective-permute-start | bytes 2359304 | tf_op jit(solution)/shard_map/ppermute | solution.py:269
  217.9 44.5 %collective-permute-start.32 = (bf16[384,1024]{1,0:T(8,128)(2,1)}, bf16[384,1024]{1,0:T(8,128)(2,1)}, u32[]{:S(2)}, u32[]{:S(2)}) collective-permute-start(bf16[384,1024]{1,0:T(8,128)(2,1)} %get-tuple-element.134), channel_id=1, source_target_pairs={{0,1},{1,0},{2,3},{3,2},{4,5},{5,4},{6,7},{7,6}} | collective-permute-start | bytes 2359304 | tf_op jit(solution)/shard_map/ppermute | solution.py:269
  217.9 24.3 %collective-permute-start.21 = (bf16[48,1024]{1,0:T(8,128)(2,1)S(1)}, bf16[48,1024]{1,0:T(8,128)(2,1)S(1)}, u32[]{:S(2)}, u32[]{:S(2)}) collective-permute-start(bf16[48,1024]{1,0:T(8,128)(2,1)S(1)} %copy-done.12), channel_id=1, source_target_pairs={{0,2},{2,0},{1,3},{3,1},{4,6},{6,4},{5,7},{7,5}} | collective-permute-start | bytes 294920 | tf_op jit(solution)/shard_map/ppermute | solution.py:269
  220.0 38.3 %collective-permute-start.24 = (bf16[96,1024]{1,0:T(8,128)(2,1)S(1)}, bf16[96,1024]{1,0:T(8,128)(2,1)S(1)}, u32[]{:S(2)}, u32[]{:S(2)}) collective-permute-start(bf16[96,1024]{1,0:T(8,128)(2,1)S(1)} %copy-done.11), channel_id=1, source_target_pairs={{0,1},{1,0},{2,3},{3,2},{4,5},{5,4},{6,7},{7,6}} | collective-permute-start | bytes 589832 | tf_op jit(solution)/shard_map/ppermute | solution.py:269
  242.3 16.8 %collective-permute-start.30 = (bf16[192,1024]{1,0:T(8,128)(2,1)}, bf16[192,1024]{1,0:T(8,128)(2,1)}, u32[]{:S(2)}, u32[]{:S(2)}) collective-permute-start(bf16[192,1024]{1,0:T(8,128)(2,1)} %get-tuple-element.133), channel_id=1, source_target_pairs={{0,2},{2,0},{1,3},{3,1},{4,6},{6,4},{5,7},{7,5}} | collective-permute-start | bytes 1179656 | tf_op jit(solution)/shard_map/ppermute | solution.py:269
  244.0 14.8 %collective-permute-start.22 = (bf16[48,1024]{1,0:T(8,128)(2,1)S(1)}, bf16[48,1024]{1,0:T(8,128)(2,1)S(1)}, u32[]{:S(2)}, u32[]{:S(2)}) collective-permute-start(bf16[48,1024]{1,0:T(8,128)(2,1)S(1)} %collective-permute-done.21.refs_0_), channel_id=1, source_target_pairs={{0,1},{1,0},{2,3},{3,2},{4,5},{5,4},{6,7},{7,6}} | collective-permute-start | bytes 294920 | tf_op jit(solution)/shard_map/ppermute | solution.py:269
  258.2 2.1 collective-permute-start.29
  258.8 37.5 %collective-permute-start.9 = (bf16[256,3072]{1,0:T(8,128)(2,1)}, bf16[256,3072]{1,0:T(8,128)(2,1)S(1)}, u32[]{:S(2)}, u32[]{:S(2)}) collective-permute-start(bf16[256,3072]{1,0:T(8,128)(2,1)} %get-tuple-element.99), channel_id=1, source_target_pairs={{0,2},{2,0},{1,3},{3,1},{4,6},{6,4},{5,7},{7,5}} | collective-permute-start | bytes 4718600 | tf_op jit(solution)/shard_map/ppermute | solution.py:269
  259.1 1.6 collective-permute-start.26
  260.3 0.8 copy-start.8
  260.3 11.3 %collective-permute-start.31 = (bf16[192,1024]{1,0:T(8,128)(2,1)}, bf16[192,1024]{1,0:T(8,128)(2,1)S(1)}, u32[]{:S(2)}, u32[]{:S(2)}) collective-permute-start(bf16[192,1024]{1,0:T(8,128)(2,1)} %collective-permute-done.30.across), channel_id=1, source_target_pairs={{0,1},{1,0},{2,3},{3,2},{4,5},{5,4},{6,7},{7,6}} | collective-permute-start | bytes 1179656 | tf_op jit(solution)/shard_map/ppermute | solution.py:269
  261.1 35.2 %collective-permute-start.8 = (bf16[256,3072]{1,0:T(8,128)(2,1)}, bf16[256,3072]{1,0:T(8,128)(2,1)}, u32[]{:S(2)}, u32[]{:S(2)}) collective-permute-start(bf16[256,3072]{1,0:T(8,128)(2,1)} %get-tuple-element.99), channel_id=1, source_target_pairs={{0,1},{1,0},{2,3},{3,2},{4,5},{5,4},{6,7},{7,6}} | collective-permute-start | bytes 4718600 | tf_op jit(solution)/shard_map/ppermute | solution.py:269
  261.5 68.6 %collective-permute-start.36 = (bf16[768,1024]{1,0:T(8,128)(2,1)}, bf16[768,1024]{1,0:T(8,128)(2,1)}, u32[]{:S(2)}, u32[]{:S(2)}) collective-permute-start(bf16[768,1024]{1,0:T(8,128)(2,1)} %get-tuple-element.135), channel_id=1, source_target_pairs={{0,2},{2,0},{1,3},{3,1},{4,6},{6,4},{5,7},{7,5}} | collective-permute-start | bytes 4718600 | tf_op jit(solution)/shard_map/ppermute | solution.py:269
  262.4 68.0 %collective-permute-start.35 = (bf16[768,1024]{1,0:T(8,128)(2,1)}, bf16[768,1024]{1,0:T(8,128)(2,1)}, u32[]{:S(2)}, u32[]{:S(2)}) collective-permute-start(bf16[768,1024]{1,0:T(8,128)(2,1)} %get-tuple-element.135), channel_id=1, source_target_pairs={{0,1},{1,0},{2,3},{3,2},{4,5},{5,4},{6,7},{7,6}} | collective-permute-start | bytes 4718600 | tf_op jit(solution)/shard_map/ppermute | solution.py:269
  271.7 1.1 copy-start.9
  271.7 92.1 %collective-permute-start.17 = (bf16[256,3072]{1,0:T(8,128)(2,1)}, bf16[256,3072]{1,0:T(8,128)(2,1)}, u32[]{:S(2)}, u32[]{:S(2)}) collective-permute-start(bf16[256,3072]{1,0:T(8,128)(2,1)} %get-tuple-element.109), channel_id=1, source_target_pairs={{0,2},{2,0},{1,3},{3,1},{4,6},{6,4},{5,7},{7,5}} | collective-permute-start | bytes 4718600 | tf_op jit(solution)/shard_map/ppermute | solution.py:269
  296.3 35.8 %copy-start.2 = (bf16[256,3072]{1,0:T(8,128)(2,1)}, bf16[256,3072]{1,0:T(8,128)(2,1)S(1)}, u32[]{:S(2)}) copy-start(bf16[256,3072]{1,0:T(8,128)(2,1)S(1)} %collective-permute-done.9.across) | copy-start | bytes 4718596
  296.3 35.8 %collective-permute-start.34 = (bf16[384,1024]{1,0:T(8,128)(2,1)}, bf16[384,1024]{1,0:T(8,128)(2,1)S(1)}, u32[]{:S(2)}, u32[]{:S(2)}) collective-permute-start(bf16[384,1024]{1,0:T(8,128)(2,1)} %collective-permute-done.33.across), channel_id=1, source_target_pairs={{0,1},{1,0},{2,3},{3,2},{4,5},{5,4},{6,7},{7,6}} | collective-permute-start | bytes 2359304 | tf_op jit(solution)/shard_map/ppermute | solution.py:269
  296.3 67.5 %collective-permute-start.16 = (bf16[256,3072]{1,0:T(8,128)(2,1)}, bf16[256,3072]{1,0:T(8,128)(2,1)}, u32[]{:S(2)}, u32[]{:S(2)}) collective-permute-start(bf16[256,3072]{1,0:T(8,128)(2,1)} %get-tuple-element.109), channel_id=1, source_target_pairs={{0,1},{1,0},{2,3},{3,2},{4,5},{5,4},{6,7},{7,6}} | collective-permute-start | bytes 4718600 | tf_op jit(solution)/shard_map/ppermute | solution.py:269
  330.1 67.4 %collective-permute-start.14 = (bf16[256,3072]{1,0:T(8,128)(2,1)}, bf16[256,3072]{1,0:T(8,128)(2,1)}, u32[]{:S(2)}, u32[]{:S(2)}) collective-permute-start(bf16[256,3072]{1,0:T(8,128)(2,1)} %get-tuple-element.108), channel_id=1, source_target_pairs={{0,2},{2,0},{1,3},{3,1},{4,6},{6,4},{5,7},{7,5}} | collective-permute-start | bytes 4718600 | tf_op jit(solution)/shard_map/ppermute | solution.py:269
  330.4 99.9 %collective-permute-start.6 = (bf16[256,3072]{1,0:T(8,128)(2,1)}, bf16[256,3072]{1,0:T(8,128)(2,1)}, u32[]{:S(2)}, u32[]{:S(2)}) collective-permute-start(bf16[256,3072]{1,0:T(8,128)(2,1)} %get-tuple-element.98), channel_id=1, source_target_pairs={{0,2},{2,0},{1,3},{3,1},{4,6},{6,4},{5,7},{7,5}} | collective-permute-start | bytes 4718600 | tf_op jit(solution)/shard_map/ppermute | solution.py:269
  332.1 105.2 %copy-start.7 = (bf16[384,1024]{1,0:T(8,128)(2,1)}, bf16[384,1024]{1,0:T(8,128)(2,1)S(1)}, u32[]{:S(2)}) copy-start(bf16[384,1024]{1,0:T(8,128)(2,1)S(1)} %collective-permute-done.34.corner) | copy-start | bytes 2359300
  332.1 98.2 %collective-permute-start.10 = (bf16[256,3072]{1,0:T(8,128)(2,1)S(1)}, bf16[256,3072]{1,0:T(8,128)(2,1)S(1)}, u32[]{:S(2)}, u32[]{:S(2)}) collective-permute-start(bf16[256,3072]{1,0:T(8,128)(2,1)S(1)} %collective-permute-done.9.across), channel_id=1, source_target_pairs={{0,1},{1,0},{2,3},{3,2},{4,5},{5,4},{6,7},{7,6}} | collective-permute-start | bytes 4718600 | tf_op jit(solution)/shard_map/ppermute | solution.py:269
  363.8 67.0 %collective-permute-start.37 = (bf16[768,1024]{1,0:T(8,128)(2,1)}, bf16[768,1024]{1,0:T(8,128)(2,1)S(1)}, u32[]{:S(2)}, u32[]{:S(2)}) collective-permute-start(bf16[768,1024]{1,0:T(8,128)(2,1)} %collective-permute-done.36.across), channel_id=1, source_target_pairs={{0,1},{1,0},{2,3},{3,2},{4,5},{5,4},{6,7},{7,6}} | collective-permute-start | bytes 4718600 | tf_op jit(solution)/shard_map/ppermute | solution.py:269
  363.8 67.6 %collective-permute-start.18 = (bf16[256,3072]{1,0:T(8,128)(2,1)}, bf16[256,3072]{1,0:T(8,128)(2,1)S(1)}, u32[]{:S(2)}, u32[]{:S(2)}) collective-permute-start(bf16[256,3072]{1,0:T(8,128)(2,1)} %collective-permute-done.17.across), channel_id=1, source_target_pairs={{0,1},{1,0},{2,3},{3,2},{4,5},{5,4},{6,7},{7,6}} | collective-permute-start | bytes 4718600 | tf_op jit(solution)/shard_map/ppermute | solution.py:269
  397.5 53.5 %collective-permute-start.13 = (bf16[256,3072]{1,0:T(8,128)(2,1)}, bf16[256,3072]{1,0:T(8,128)(2,1)}, u32[]{:S(2)}, u32[]{:S(2)}) collective-permute-start(bf16[256,3072]{1,0:T(8,128)(2,1)} %get-tuple-element.108), channel_id=1, source_target_pairs={{0,1},{1,0},{2,3},{3,2},{4,5},{5,4},{6,7},{7,6}} | collective-permute-start | bytes 4718600 | tf_op jit(solution)/shard_map/ppermute | solution.py:269
  430.3 20.7 %collective-permute-start.15 = (bf16[256,3072]{1,0:T(8,128)(2,1)}, bf16[256,3072]{1,0:T(8,128)(2,1)}, u32[]{:S(2)}, u32[]{:S(2)}) collective-permute-start(bf16[256,3072]{1,0:T(8,128)(2,1)} %collective-permute-done.14.across), channel_id=1, source_target_pairs={{0,1},{1,0},{2,3},{3,2},{4,5},{5,4},{6,7},{7,6}} | collective-permute-start | bytes 4718600 | tf_op jit(solution)/shard_map/ppermute | solution.py:269
  430.3 1.2 copy-start.4
  430.3 25.0 %collective-permute-start.5 = (bf16[256,3072]{1,0:T(8,128)(2,1)}, bf16[256,3072]{1,0:T(8,128)(2,1)S(1)}, u32[]{:S(2)}, u32[]{:S(2)}) collective-permute-start(bf16[256,3072]{1,0:T(8,128)(2,1)} %get-tuple-element.98), channel_id=1, source_target_pairs={{0,1},{1,0},{2,3},{3,2},{4,5},{5,4},{6,7},{7,6}} | collective-permute-start | bytes 4718600 | tf_op jit(solution)/shard_map/ppermute | solution.py:269
  430.8 1.2 copy-start.6
  430.8 24.5 %collective-permute-start.7 = (bf16[256,3072]{1,0:T(8,128)(2,1)}, bf16[256,3072]{1,0:T(8,128)(2,1)}, u32[]{:S(2)}, u32[]{:S(2)}) collective-permute-start(bf16[256,3072]{1,0:T(8,128)(2,1)} %collective-permute-done.6.across), channel_id=1, source_target_pairs={{0,1},{1,0},{2,3},{3,2},{4,5},{5,4},{6,7},{7,6}} | collective-permute-start | bytes 4718600 | tf_op jit(solution)/shard_map/ppermute | solution.py:269
  432.0 1.1 copy-start.5
  433.2 21.5 %collective-permute-start.38 = (bf16[48,1024]{1,0:T(8,128)(2,1)S(1)}, bf16[48,1024]{1,0:T(8,128)(2,1)S(1)}, u32[]{:S(2)}, u32[]{:S(2)}) collective-permute-start(bf16[48,1024]{1,0:T(8,128)(2,1)S(1)} %collective-permute-done.23.refs_2_), channel_id=1, source_target_pairs={{0,1},{1,0},{2,3},{3,2},{4,5},{5,4},{6,7},{7,6}} | collective-permute-start | bytes 294920 | tf_op jit(solution)/shard_map/ppermute | solution.py:269
  455.3 1.2 copy-start.3
